TPU v7x, 512 devices: a whole 4x4x16 slice. The times are simulated.
512 devices in a mesh: dp: 16 (over z_lo, core), block: 32 (over y, z_hi, x).
Axes of the slice: x: 4, y: 4, z: 16 (z_hi: 2, z_lo: 8; z = z_hi * 8 + z_lo), core: 2. Of those that a mesh axis runs over, the one named last changes fastest.
Arguments:
- tokens: bfloat16 [4096, 16384], P('dp', 'block'), may hold values from -6 to 6
- upper_left: bfloat16 [64, 256, 1024], P('block', 'dp'), may hold values from -0.375 to 0.375
- upper_right: bfloat16 [256, 256, 256], P('block', 'dp'), may hold values from -0.375 to 0.375
- lower_right: bfloat16 [256, 256, 256], P('block', 'dp'), may hold values from -0.375 to 0.375
- lower_left: bfloat16 [64, 1024, 256], P('block', 'dp'), may hold values from -0.1875 to 0.1875
- cotangent: bfloat16 [4096, 16384], P('dp', 'block'), may hold values from -6 to 6
Outputs:
- output: bfloat16 [4096, 16384], P('dp', 'block')
- token_grad: bfloat16 [4096, 16384], P('dp', 'block')
- upper_left_grad: float32 [64, 256, 1024], P('block', 'dp')
- upper_right_grad: float32 [256, 256, 256], P('block', 'dp')
- lower_right_grad: float32 [256, 256, 256], P('block', 'dp')
- lower_left_grad: float32 [64, 1024, 256], P('block', 'dp')
All inputs are finite; a program needn't handle non-finite values.
Results may differ from a plain program's by a relative error of at most 0.017.
Values may be sent and summed in bfloat16 or wider, within the bound.
A program may use at most 64 MiB of HBM per device.

v0:
```python
import jax
import jax.numpy as jnp
from jax import lax
from jax.sharding import PartitionSpec as P


def contract(form, left, right):
    return jnp.einsum(form, left, right, preferred_element_type=jnp.float32)


def permute(values):
    return lax.all_to_all(values, "block", split_axis=1, concat_axis=0, tiled=True)


def forward(tokens, weights, mover):
    in_left, in_right, out_right, out_left = weights
    width = in_right.shape[1]
    rows = tokens.shape[0]
    local_blocks = in_left.shape[0]
    expand = in_left.shape[2] // width
    x_three = tokens.reshape(rows, local_blocks, width)
    left_four = in_left.reshape(local_blocks, width, expand, width)
    mixed = (
        contract("tkb,kbec->kect", x_three, left_four)
        .astype(jnp.bfloat16)
        .reshape(local_blocks * expand, width, rows)
    )
    spread = mover(mixed)
    hidden_pre = contract("act,cab->cbt", spread, in_right)
    active = jax.nn.gelu(hidden_pre).astype(jnp.bfloat16)
    narrow = contract("cbt,cbe->cet", active, out_right).astype(jnp.bfloat16)
    gathered = mover(narrow)
    narrow_four = gathered.reshape(width, local_blocks, expand, rows)
    out_four = out_left.reshape(local_blocks, expand, width, width)
    result = (
        contract("ckft,kfco->tko", narrow_four, out_four)
        .astype(jnp.bfloat16)
        .reshape(rows, local_blocks * width)
    )
    return (result, spread, hidden_pre, active, narrow_four)


def local(tokens, upper_left, upper_right, lower_right, lower_left, cotangent):
    weights = (
        lax.all_gather(upper_left, "dp", axis=1, tiled=True),
        lax.all_gather(upper_right, "dp", axis=1, tiled=True),
        lax.all_gather(lower_right, "dp", axis=1, tiled=True),
        lax.all_gather(lower_left, "dp", axis=1, tiled=True),
    )
    in_left, in_right, out_right, out_left = weights
    width = in_right.shape[1]
    rows = tokens.shape[0]
    local_blocks = in_left.shape[0]
    expand = in_left.shape[2] // width
    result, spread, hidden_pre, active, narrow_four = forward(tokens, weights, permute)
    x_three = tokens.reshape(rows, local_blocks, width)
    left_four = in_left.reshape(local_blocks, width, expand, width)
    out_four = out_left.reshape(local_blocks, expand, width, width)
    cot_three = cotangent.reshape(rows, local_blocks, width)
    grad_lower_left = contract("ckft,tko->kfco", narrow_four, cot_three).reshape(
        local_blocks, expand * width, width
    )
    back_narrow = (
        contract("tko,kfco->kfct", cot_three, out_four)
        .astype(jnp.bfloat16)
        .reshape(local_blocks * expand, width, rows)
    )
    narrow_back = permute(back_narrow)
    grad_lower_right = contract("cbt,ect->cbe", active, narrow_back)
    back_active = contract("ect,cbe->cbt", narrow_back, out_right)
    back_pre = jax.vjp(jax.nn.gelu, hidden_pre)[1](back_active)[0].astype(jnp.bfloat16)
    grad_upper_right = contract("act,cbt->cab", spread, back_pre)
    back_mixed = contract("cbt,cab->cat", back_pre, in_right).astype(jnp.bfloat16)
    mixed_back = permute(back_mixed).reshape(width, local_blocks, expand, rows)
    grad_upper_left = contract("tkb,cket->kbec", x_three, mixed_back).reshape(
        local_blocks, width, expand * width
    )
    token_grad = (
        contract("cket,kbec->tkb", mixed_back, left_four)
        .astype(jnp.bfloat16)
        .reshape(rows, local_blocks * width)
    )
    grad_upper_left, grad_upper_right, grad_lower_right, grad_lower_left = (
        lax.psum_scatter(
            grad_upper_left.astype(jnp.bfloat16), "dp", scatter_dimension=1, tiled=True
        ).astype(jnp.float32),
        lax.psum_scatter(
            grad_upper_right.astype(jnp.bfloat16), "dp", scatter_dimension=1, tiled=True
        ).astype(jnp.float32),
        lax.psum_scatter(
            grad_lower_right.astype(jnp.bfloat16), "dp", scatter_dimension=1, tiled=True
        ).astype(jnp.float32),
        lax.psum_scatter(
            grad_lower_left.astype(jnp.bfloat16), "dp", scatter_dimension=1, tiled=True
        ).astype(jnp.float32),
    )
    return (
        result,
        token_grad,
        grad_upper_left,
        grad_upper_right,
        grad_lower_right,
        grad_lower_left,
    )


def solution(mesh):
    in_specs = (
        P("dp", "block"),
        P("block", "dp", None),
        P("block", "dp", None),
        P("block", "dp", None),
        P("block", "dp", None),
        P("dp", "block"),
    )
    out_specs = (
        P("dp", "block"),
        P("dp", "block"),
        P("block", "dp", None),
        P("block", "dp", None),
        P("block", "dp", None),
        P("block", "dp", None),
    )
    return jax.shard_map(local, mesh=mesh, in_specs=in_specs, out_specs=out_specs, check_vma=False)
```

profile of v0, /device:TPU:6, one launch (start us, length us, event | category | flops | bytes accessed | tf_op | source)
XLA Modules:
  0.0 939.5 jit_solution(8600866587322765931)
XLA Ops:
  8.9 104.0 %all-gather.5.cloned.1.call-done = bf16[2,256,1024]{2,1,0:T(8,128)(2,1)} async-done(((bf16[2,16,1024]{2,1,0:T(8,128)(2,1)}), bf16[2,256,1024]{2,1,0:T(8,128)(2,1)}) %all-gather.5.cloned.1.call-update) | async-done | bytes 1048592 | tf_op jit(solution)/shard_map/all_gather | solution.py:45
  112.9 1.5 copy.72
  114.8 1.6 copy.74
  116.4 18.3 %all-to-all-start = ((bf16[8,256,256]{2,0,1:T(8,128)(2,1)}), bf16[8,256,256]{2,0,1:T(8,128)(2,1)S(1)}, u32[]{:S(2)}, u32[]{:S(2)}) async-start(bf16[8,256,256]{2,0,1:T(8,128)(2,1)} %copy.74), calls=%async_computation | async-start | bytes 2097152 | tf_op jit(solution)/shard_map/all_to_all | solution.py:12
  135.6 102.4 %all-gather.11.cloned.1.call-done = bf16[2,1024,256]{2,1,0:T(8,128)(2,1)} async-done(((bf16[2,64,256]{2,1,0:T(8,128)(2,1)}), bf16[2,1024,256]{2,1,0:T(8,128)(2,1)}) %all-gather.11.cloned.1.call-update) | async-done | bytes 1048592 | tf_op jit(solution)/shard_map/all_gather | solution.py:48
  238.0 1.7 convolution_convert_fusion.5
  239.7 1.6 copy.83
  241.2 16.7 %all-to-all-start.2 = ((bf16[8,256,256]{2,0,1:T(8,128)(2,1)}), bf16[8,256,256]{2,0,1:T(8,128)(2,1)}, u32[]{:S(2)}, u32[]{:S(2)}) async-start(bf16[8,256,256]{2,0,1:T(8,128)(2,1)} %copy.83), calls=%async_computation.2 | async-start | bytes 2097152 | tf_op jit(solution)/shard_map/all_to_all | solution.py:12
  259.6 26.5 %all-to-all-done.2 = bf16[8,256,256]{2,0,1:T(8,128)(2,1)} async-done(((bf16[8,256,256]{2,0,1:T(8,128)(2,1)}), bf16[8,256,256]{2,0,1:T(8,128)(2,1)}, u32[]{:S(2)}, u32[]{:S(2)}) %all-to-all-start.2) | async-done | bytes 1048608 | tf_op jit(solution)/shard_map/all_to_all | solution.py:12
  286.0 2.5 copy.85
  288.6 72.4 %all-gather.7.cloned.1.call-done = bf16[8,256,256]{2,1,0:T(8,128)(2,1)} async-done(((bf16[8,16,256]{2,1,0:T(8,128)(2,1)}), bf16[8,256,256]{2,1,0:T(8,128)(2,1)}) %all-gather.7.cloned.1.call-update) | async-done | bytes 1048592 | tf_op jit(solution)/shard_map/all_gather | solution.py:46
  361.0 3.1 fusion.17
  364.1 97.4 %all-gather.9.cloned.1.call-done = bf16[8,256,256]{2,1,0:T(8,128)(2,1)} async-done(((bf16[8,16,256]{2,1,0:T(8,128)(2,1)}), bf16[8,256,256]{2,1,0:T(8,128)(2,1)}) %all-gather.9.cloned.1.call-update) | async-done | bytes 1048592 | tf_op jit(solution)/shard_map/all_gather | solution.py:47
  461.5 4.0 fusion.6
  467.0 2.7 copy.87
  469.7 17.5 %all-to-all-start.3 = ((bf16[8,256,256]{2,0,1:T(8,128)(2,1)}), bf16[8,256,256]{2,0,1:T(8,128)(2,1)}, u32[]{:S(2)}, u32[]{:S(2)}) async-start(bf16[8,256,256]{2,0,1:T(8,128)(2,1)} %copy.87), calls=%async_computation.3 | async-start | bytes 2097152 | tf_op jit(solution)/shard_map/all_to_all | solution.py:12
  488.7 2.7 fusion.11
  491.4 1.8 copy.78
  493.2 25.6 %all-to-all-done.3 = bf16[8,256,256]{2,0,1:T(8,128)(2,1)} async-done(((bf16[8,256,256]{2,0,1:T(8,128)(2,1)}), bf16[8,256,256]{2,0,1:T(8,128)(2,1)}, u32[]{:S(2)}, u32[]{:S(2)}) %all-to-all-start.3) | async-done | bytes 1048608 | tf_op jit(solution)/shard_map/all_to_all | solution.py:12
  518.9 21.3 %all-to-all-start.1 = ((bf16[8,256,256]{2,0,1:T(8,128)(2,1)}), bf16[8,256,256]{2,0,1:T(8,128)(2,1)S(1)}, u32[]{:S(2)}, u32[]{:S(2)}) async-start(bf16[8,256,256]{2,0,1:T(8,128)(2,1)} %copy.78), calls=%async_computation.1 | async-start | bytes 2097152 | tf_op jit(solution)/shard_map/all_to_all | solution.py:12
  540.3 3.7 convolution_convert_fusion.1
  546.9 2.3 copy.92
  549.3 25.5 %all-to-all-done.1 = bf16[8,256,256]{2,0,1:T(8,128)(2,1)S(1)} async-done(((bf16[8,256,256]{2,0,1:T(8,128)(2,1)}), bf16[8,256,256]{2,0,1:T(8,128)(2,1)S(1)}, u32[]{:S(2)}, u32[]{:S(2)}) %all-to-all-start.1) | async-done | bytes 1048608 | tf_op jit(solution)/shard_map/all_to_all | solution.py:12
  578.5 37.8 %reduce-scatter.7.cloned.1.call-done = bf16[8,16,256]{2,1,0:T(8,128)(2,1)} async-done(((bf16[8,256,256]{2,1,0:T(8,128)(2,1)}), bf16[8,16,256]{2,1,0:T(8,128)(2,1)}) %reduce-scatter.7.cloned.1.call-update) | async-done | bytes 65552 | tf_op jit(solution)/shard_map/reduce_scatter | solution.py:87
  616.2 1.5 convert_element_type.89
  617.8 106.2 %reduce-scatter.9.cloned.1.call-done = bf16[8,16,256]{2,1,0:T(8,128)(2,1)} async-done(((bf16[8,256,256]{2,1,0:T(8,128)(2,1)}), bf16[8,16,256]{2,1,0:T(8,128)(2,1)}) %reduce-scatter.9.cloned.1.call-update) | async-done | bytes 65552 | tf_op jit(solution)/shard_map/reduce_scatter | solution.py:90
  723.9 1.5 convert_element_type.91
  725.5 1.7 fusion.13
  729.4 98.0 %reduce-scatter.5.cloned.1.call-done = bf16[2,16,1024]{2,1,0:T(8,128)(2,1)} async-done(((bf16[2,256,1024]{2,1,0:T(8,128)(2,1)}), bf16[2,16,1024]{2,1,0:T(8,128)(2,1)}) %reduce-scatter.5.cloned.1.call-update) | async-done | bytes 65552 | tf_op jit(solution)/shard_map/reduce_scatter | solution.py:84
  827.4 1.5 convert_element_type.87
  829.0 102.2 %reduce-scatter.11.cloned.1.call-done = bf16[2,64,256]{2,1,0:T(8,128)(2,1)} async-done(((bf16[2,1024,256]{2,1,0:T(8,128)(2,1)}), bf16[2,64,256]{2,1,0:T(8,128)(2,1)}) %reduce-scatter.11.cloned.1.call-update) | async-done | bytes 65552 | tf_op jit(solution)/shard_map/reduce_scatter | solution.py:93
  931.1 1.5 convert_element_type.95
  (42 shorter events, 16.5 us)
Async XLA Ops:
  7.2 105.7 %all-gather.5.cloned.1.call-start = ((), (), s32[]{:S(2)}) async-start(), calls=%async_computation.8 | async-start | bytes 1114112 | tf_op jit(solution)/shard_map/all_gather | solution.py:45
  114.8 20.7 %copy-start.5 = (bf16[256,512]{1,0:T(8,128)(2,1)S(1)}, bf16[256,512]{1,0:T(8,128)(2,1)}, u32[]{:S(2)}) copy-start(bf16[256,512]{1,0:T(8,128)(2,1)} %param.11) | copy-start | bytes 786436
  116.4 124.8 %all-to-all-start = ((bf16[8,256,256]{2,0,1:T(8,128)(2,1)}), bf16[8,256,256]{2,0,1:T(8,128)(2,1)S(1)}, u32[]{:S(2)}, u32[]{:S(2)}) async-start(bf16[8,256,256]{2,0,1:T(8,128)(2,1)} %copy.74), calls=%async_computation | async-start | bytes 2097152 | tf_op jit(solution)/shard_map/all_to_all | solution.py:12
  134.7 103.2 %all-gather.11.cloned.1.call-start = ((), (), s32[]{:S(2)}) async-start(), calls=%async_computation.11 | async-start | bytes 1114112 | tf_op jit(solution)/shard_map/all_gather | solution.py:48
  135.6 105.7 %copy-start.2 = (bf16[256,2,256]{2,1,0:T(2,128)(2,1)}, bf16[256,2,256]{2,1,0:T(2,128)(2,1)S(1)}, u32[]{:S(2)}) copy-start(bf16[256,2,256]{2,1,0:T(2,128)(2,1)S(1)} %reshape.57) | copy-start | bytes 786436
  241.2 44.8 %all-to-all-start.2 = ((bf16[8,256,256]{2,0,1:T(8,128)(2,1)}), bf16[8,256,256]{2,0,1:T(8,128)(2,1)}, u32[]{:S(2)}, u32[]{:S(2)}) async-start(bf16[8,256,256]{2,0,1:T(8,128)(2,1)} %copy.83), calls=%async_computation.2 | async-start | bytes 2097152 | tf_op jit(solution)/shard_map/all_to_all | solution.py:12
  257.9 103.1 %all-gather.7.cloned.1.call-start = ((), (), s32[]{:S(2)}) async-start(), calls=%async_computation.9 | async-start | bytes 1114112 | tf_op jit(solution)/shard_map/all_gather | solution.py:46
  258.7 202.8 %all-gather.9.cloned.1.call-start = ((), (), s32[]{:S(2)}) async-start(), calls=%async_computation.10 | async-start | bytes 1114112 | tf_op jit(solution)/shard_map/all_gather | solution.py:47
  461.5 4.0 copy-start.1
  469.7 49.2 %all-to-all-start.3 = ((bf16[8,256,256]{2,0,1:T(8,128)(2,1)}), bf16[8,256,256]{2,0,1:T(8,128)(2,1)}, u32[]{:S(2)}, u32[]{:S(2)}) async-start(bf16[8,256,256]{2,0,1:T(8,128)(2,1)} %copy.87), calls=%async_computation.3 | async-start | bytes 2097152 | tf_op jit(solution)/shard_map/all_to_all | solution.py:12
  487.2 129.0 %reduce-scatter.7.cloned.1.call-start = ((), (), s32[]{:S(2)}) async-start(), calls=%async_computation.13 | async-start | bytes 1114112 | tf_op jit(solution)/shard_map/reduce_scatter | solution.py:87
  491.4 48.8 %copy-start.4 = (bf16[32,8,8,256]{3,2,1,0:T(8,128)(2,1)S(1)}, bf16[32,8,8,256]{3,2,1,0:T(8,128)(2,1)}, u32[]{:S(2)}) copy-start(bf16[32,8,8,256]{3,2,1,0:T(8,128)(2,1)} %copy.85) | copy-start | bytes 3145732
  518.9 55.9 %all-to-all-start.1 = ((bf16[8,256,256]{2,0,1:T(8,128)(2,1)}), bf16[8,256,256]{2,0,1:T(8,128)(2,1)S(1)}, u32[]{:S(2)}, u32[]{:S(2)}) async-start(bf16[8,256,256]{2,0,1:T(8,128)(2,1)} %copy.78), calls=%async_computation.1 | async-start | bytes 2097152 | tf_op jit(solution)/shard_map/all_to_all | solution.py:12
  540.2 183.7 %reduce-scatter.9.cloned.1.call-start = ((), (), s32[]{:S(2)}) async-start(), calls=%async_computation.14 | async-start | bytes 1114112 | tf_op jit(solution)/shard_map/reduce_scatter | solution.py:90
  544.0 283.5 %reduce-scatter.5.cloned.1.call-start = ((), (), s32[]{:S(2)}) async-start(), calls=%async_computation.12 | async-start | bytes 1114112 | tf_op jit(solution)/shard_map/reduce_scatter | solution.py:84
  549.2 27.8 %copy-start.3 = (bf16[256,2,256]{2,1,0:T(2,128)(2,1)S(1)}, bf16[256,2,256]{2,1,0:T(2,128)(2,1)}, u32[]{:S(2)}) copy-start(bf16[256,2,256]{2,1,0:T(2,128)(2,1)} %copy-done.2) | copy-start | bytes 786436
  549.2 381.9 %reduce-scatter.11.cloned.1.call-start = ((), (), s32[]{:S(2)}) async-start(), calls=%async_computation.15 | async-start | bytes 1114112 | tf_op jit(solution)/shard_map/reduce_scatter | solution.py:93
  574.8 1.0 copy-start
Sparse Core Ops, SparseCore 0:
  10.1 102.7 all-gather.4
  137.6 100.2 all-gather.10
  260.8 100.1 all-gather.6
  363.0 98.5 all-gather.8
  490.5 125.6 reduce-scatter.6
  618.9 104.9 reduce-scatter.8
  726.8 100.6 reduce-scatter.4
  830.2 100.8 reduce-scatter.10
where the time goes:
time: 941 us; the launch traced here: 939 us
  waiting for transfers between devices  801 us (85%)
  starting transfers between devices  74.4 us (8%)
  matrix products  23.5 us (2%)
  local copies, waits for them, and re-layouts  20.6 us (2%)
  between operations  14.3 us (2%)
    reduce_scatter x1, waiting for transfers between devices, local(): lax.psum_scatter(grad_lower_right.astype(jnp.bfloat16), 'dp', scatter_dim...  106 us
    all_gather x1, waiting for transfers between devices, local(): lax.all_gather(upper_left, 'dp', axis=1, tiled=True)  104 us
    all_gather x1, waiting for transfers between devices, local(): lax.all_gather(lower_left, 'dp', axis=1, tiled=True)  102 us
    reduce_scatter x1, waiting for transfers between devices, local(): lax.psum_scatter(grad_lower_left.astype(jnp.bfloat16), 'dp', scatter_dime...  102 us
    reduce_scatter x1, waiting for transfers between devices, local(): lax.psum_scatter(grad_upper_left.astype(jnp.bfloat16), 'dp', scatter_dime...  98 us
    all_gather x1, waiting for transfers between devices, local(): lax.all_gather(lower_right, 'dp', axis=1, tiled=True)  97.4 us
    all_to_all x4, waiting for transfers between devices, permute(): lax.all_to_all(values, 'block', split_axis=1, concat_axis=0, tiled=True)  77.6 us
    all_to_all x4, starting transfers between devices, permute(): lax.all_to_all(values, 'block', split_axis=1, concat_axis=0, tiled=True)  73.9 us
  transfers between devices with their start and end apart: 12, of which 11 were waited for; matrix products, arithmetic and copies ran while one was open for 4% of the time, Pallas kernels for 0%

commit v1 on v0

v1 whole, which is shorter than its diff:
```python
import functools

import jax
import jax.numpy as jnp
from jax import lax
from jax.experimental import pallas as pl
from jax.experimental.pallas import tpu as pltpu
from jax.sharding import PartitionSpec as P

ZL, CORES, NY, ZH, NX = 8, 2, 4, 2, 4
RING = ZL * ZH
BF = jnp.bfloat16
F32 = jnp.float32


def contract(form, left, right):
    return jnp.einsum(form, left, right, preferred_element_type=F32)


def place():
    dp = lax.axis_index("dp")
    block = lax.axis_index("block")
    zl, core = dp // CORES, dp % CORES
    y, rest = block // (ZH * NX), block % (ZH * NX)
    zh, x = rest // NX, rest % NX
    return zl, core, y, zh, x


def at(z, core, y, x):
    z = z % RING
    return {
        "dp": (z % ZL) * CORES + core,
        "block": y * (ZH * NX) + (z // ZL) * NX + x,
    }


def greet(z, core, y, x):
    barrier = pltpu.get_barrier_semaphore()
    for who in (at(z + 1, core, y, x), at(z + RING - 1, core, y, x), at(z, 1 - core, y, x)):
        pl.semaphore_signal(barrier, inc=1, device_id=who, device_id_type=pl.DeviceIdType.MESH)
    pl.semaphore_wait(barrier, 3)


def gather_kernel(count, *refs):
    own, out = refs[:count], refs[count : 2 * count]
    send, recv, local = refs[2 * count :]
    zl, core, y, zh, x = place()
    z = zh * ZL + zl
    right, left = at(z + 1, core, y, x), at(z + RING - 1, core, y, x)
    other = at(z, 1 - core, y, x)
    greet(z, core, y, x)

    def spot(w, source):
        source = source % RING
        return out[w].at[source // ZL, :, source % ZL, core]

    def push(w, slot, source, target, src=None):
        where = spot(w, source)
        copy = pltpu.make_async_remote_copy(
            src_ref=where if src is None else src,
            dst_ref=where,
            send_sem=send.at[w, slot],
            recv_sem=recv.at[w, slot],
            device_id=target,
            device_id_type=pl.DeviceIdType.MESH,
        )
        copy.start()
        return copy

    half = RING // 2
    sent = []
    rights, lefts, keeps = [], [], []
    for w in range(count):
        src = own[w]
        rights.append(push(w, 0, z, right, src))
        lefts.append(push(w, half, z, left, src))
        sent.append(push(w, RING - 1, z, other, src))
        keep = pltpu.make_async_copy(src, spot(w, z), local.at[w])
        keep.start()
        keeps.append(keep)
    for s in range(1, half + 1):
        for w in range(count):
            rights[w].wait_recv()
            sent.append(rights[w])
            if s < half:
                rights[w] = push(w, s, z + RING - s, right)
            sent.append(push(w, RING + s, z + RING - s, other))
            if s < half:
                lefts[w].wait_recv()
                sent.append(lefts[w])
                if s < half - 1:
                    lefts[w] = push(w, half + s, z + s, left)
                sent.append(push(w, RING + half + s, z + s, other))
    mirrors = [
        (w, slot)
        for w in range(count)
        for slot in [RING - 1] + list(range(RING + 1, RING + half + half))
    ]
    for w, slot in mirrors:
        pltpu.make_async_remote_copy(
            src_ref=own[w],
            dst_ref=own[w],
            send_sem=send.at[w, slot],
            recv_sem=recv.at[w, slot],
            device_id=other,
            device_id_type=pl.DeviceIdType.MESH,
        ).wait_recv()
    for copy in sent:
        copy.wait_send()
    for keep in keeps:
        keep.wait()


def ring_gather(shards, collective_id):
    count = len(shards)
    slots = 2 * RING
    shapes = [
        jax.ShapeDtypeStruct((ZH, s.shape[0], ZL, CORES) + s.shape[1:], s.dtype) for s in shards
    ]
    outs = pl.pallas_call(
        functools.partial(gather_kernel, count),
        out_shape=shapes,
        in_specs=[pl.BlockSpec(memory_space=pltpu.VMEM)] * count,
        out_specs=[pl.BlockSpec(memory_space=pl.ANY)] * count,
        scratch_shapes=[
            pltpu.SemaphoreType.DMA((count, slots)),
            pltpu.SemaphoreType.DMA((count, slots)),
            pltpu.SemaphoreType.DMA((count,)),
        ],
        compiler_params=pltpu.CompilerParams(collective_id=collective_id, has_side_effects=True),
        name="ring_gather",
    )(*shards)
    return [
        o.reshape(ZH * s.shape[0], ZL * CORES * s.shape[1], s.shape[2])
        for o, s in zip(outs, shards)
    ]


def scatter_kernel(count, *refs):
    part, out = refs[:count], refs[count : 2 * count]
    rest = refs[2 * count :]
    mate, come, stage = rest[:count], rest[count : 2 * count], rest[2 * count : 3 * count]
    send, recv, msend, mrecv = rest[3 * count :]
    zl, core, y, zh, x = place()
    z = zh * ZL + zl
    right, left = at(z + 1, core, y, x), at(z + RING - 1, core, y, x)
    other = at(z, 1 - core, y, x)
    greet(z, core, y, x)
    half = RING // 2

    def goal(slot):
        if slot < half:
            return (z + half - slot) % RING
        return (z + RING - (half - 1) + (slot - half)) % RING

    order = []
    for s in range(half):
        order.append(s)
        if half + s < RING - 1:
            order.append(half + s)
    order.append(RING - 1)

    mates = {}
    for slot in order:
        d = goal(slot)
        for w in range(count):
            copy = pltpu.make_async_remote_copy(
                src_ref=part[w].at[d // ZL, :, d % ZL, 1 - core],
                dst_ref=mate[w].at[slot],
                send_sem=msend.at[w, slot],
                recv_sem=mrecv.at[w, slot],
                device_id=other,
                device_id_type=pl.DeviceIdType.MESH,
            )
            copy.start()
            mates[w, slot] = copy
    moves = {}
    for slot in order:
        d = goal(slot)
        for w in range(count):
            mates[w, slot].wait_recv()
            total = part[w][d // ZL, :, d % ZL, core].astype(F32) + mate[w][slot].astype(F32)
            if slot == RING - 1:
                for last in (half - 1, RING - 2):
                    moves[w, last].wait_recv()
                    total = total + come[w][last].astype(F32)
                out[w][...] = total
                continue
            if slot not in (0, half):
                moves[w, slot - 1].wait_recv()
                total = total + come[w][slot - 1].astype(F32)
            stage[w][slot] = total.astype(BF)
            copy = pltpu.make_async_remote_copy(
                src_ref=stage[w].at[slot],
                dst_ref=come[w].at[slot],
                send_sem=send.at[w, slot],
                recv_sem=recv.at[w, slot],
                device_id=right if slot < half else left,
                device_id_type=pl.DeviceIdType.MESH,
            )
            copy.start()
            moves[w, slot] = copy
    for copy in mates.values():
        copy.wait_send()
    for copy in moves.values():
        copy.wait_send()


def ring_scatter(parts, collective_id):
    count = len(parts)
    split, shards = [], []
    for p in parts:
        shard = (p.shape[0] // ZH, p.shape[1] // (ZL * CORES), p.shape[2])
        shards.append(shard)
        split.append(p.reshape(ZH, shard[0], ZL, CORES, shard[1], shard[2]))
    return pl.pallas_call(
        functools.partial(scatter_kernel, count),
        out_shape=[jax.ShapeDtypeStruct(s, F32) for s in shards],
        in_specs=[pl.BlockSpec(memory_space=pltpu.VMEM)] * count,
        out_specs=[pl.BlockSpec(memory_space=pltpu.VMEM)] * count,
        scratch_shapes=[pltpu.VMEM((RING,) + s, BF) for s in shards]
        + [pltpu.VMEM((RING - 1,) + s, BF) for s in shards]
        + [pltpu.VMEM((RING - 1,) + s, BF) for s in shards]
        + [
            pltpu.SemaphoreType.DMA((count, RING - 1)),
            pltpu.SemaphoreType.DMA((count, RING - 1)),
            pltpu.SemaphoreType.DMA((count, RING)),
            pltpu.SemaphoreType.DMA((count, RING)),
        ],
        compiler_params=pltpu.CompilerParams(
            collective_id=collective_id, has_side_effects=True, vmem_limit_bytes=56 * 2**20
        ),
        name="ring_scatter",
    )(*split)


GROUPS = [
    [y * (ZH * NX) + zh * NX + x for y in range(NY) for x in range(NX)] for zh in range(ZH)
]
SWAP = [(b, b ^ NX) for b in range(NY * ZH * NX)]


def exchange(values):
    return lax.all_to_all(
        values, "block", split_axis=0, concat_axis=0, tiled=True, axis_index_groups=GROUPS
    )


def to_columns(values):
    n, k, e, c, t = values.shape
    cols = c // (NY * ZH * NX)
    kl = k // ZH
    v = values.reshape(n, k * e, NY, ZH, NX, cols, t)
    v = v.transpose(2, 4, 0, 3, 5, 1, 6).reshape(NY * NX, n, ZH * cols, k * e, t)
    v = exchange(v)
    v = v.reshape(NY, NX, n, ZH * cols, ZH, kl * e, t)
    return v.transpose(2, 3, 0, 4, 1, 5, 6).reshape(n, ZH * cols, NY * NX * k * e, t)


def to_rows(values, kl):
    n, c, a, t = values.shape
    rows = a // (NY * ZH * NX)
    cols = c // ZH
    v = values.reshape(n, c, NY, ZH, NX, rows, t)
    v = v.transpose(2, 4, 0, 3, 5, 1, 6).reshape(NY * NX, n, ZH * rows, c, t)
    v = exchange(v)
    v = v.reshape(NY, NX, n, ZH * rows, ZH, cols, t)
    v = v.transpose(2, 3, 0, 4, 1, 5, 6)
    return v.reshape(n, ZH * kl, rows // kl, NY * NX * c, t)


def local(tokens, upper_left, upper_right, lower_right, lower_left, cotangent):
    zl, core, y, zh, x = place()
    rows, features = tokens.shape
    width = upper_left.shape[1] * ZL * CORES
    kl = upper_left.shape[0]
    expand = upper_left.shape[2] // width
    few = rows // ZH
    low = zh == 0

    both = jnp.stack([tokens, cotangent]).reshape(2, ZH, few, features)
    mine = jnp.where(low, both[:, 0], both[:, 1])
    away = jnp.where(low, both[:, 1], both[:, 0])
    came = lax.ppermute(away, "block", SWAP)
    pair = jnp.stack([jnp.where(low, mine, came), jnp.where(low, came, mine)], axis=2)
    pair = pair.reshape(2, few, ZH * kl, width)
    toks, cots = pair[0], pair[1]

    in_left, out_left, in_right, out_right = ring_gather(
        (upper_left, lower_left, upper_right, lower_right), 1
    )
    left_four = in_left.reshape(ZH * kl, width, expand, width)
    out_four = out_left.reshape(ZH * kl, expand, width, width)

    mixed = contract("tkb,kbec->kect", toks, left_four).astype(BF)
    back_narrow = contract("tko,kfco->kfct", cots, out_four).astype(BF)
    columns = to_columns(jnp.stack([mixed, back_narrow]))
    spread, narrow_back = columns[0], columns[1]

    hidden_pre = contract("cat,cab->cbt", spread, in_right)
    active = jax.nn.gelu(hidden_pre).astype(BF)
    narrow = contract("cbt,cbe->cet", active, out_right).astype(BF)
    back_active = contract("cet,cbe->cbt", narrow_back, out_right)
    back_pre = jax.vjp(jax.nn.gelu, hidden_pre)[1](back_active)[0].astype(BF)
    back_mixed = contract("cbt,cab->cat", back_pre, in_right).astype(BF)
    rowed = to_rows(jnp.stack([narrow, back_mixed]), kl)
    narrow_four, mixed_back = rowed[0], rowed[1]

    grad_lower_right = contract("cbt,cet->cbe", active, narrow_back).astype(BF)
    grad_upper_right = contract("cat,cbt->cab", spread, back_pre).astype(BF)
    result = contract("kfct,kfco->tko", narrow_four, out_four).astype(BF)
    token_grad = contract("kect,kbec->tkb", mixed_back, left_four).astype(BF)

    ends = jnp.stack([result, token_grad]).reshape(2, few, ZH, features)
    keep = jnp.where(low, ends[:, :, 0], ends[:, :, 1])
    away = jnp.where(low, ends[:, :, 1], ends[:, :, 0])
    came = lax.ppermute(away, "block", SWAP)
    ends = jnp.concatenate([jnp.where(low, keep, came), jnp.where(low, came, keep)], axis=1)

    grad_lower_left = contract("kfct,tko->kfco", narrow_four, cots).astype(BF)
    grad_upper_left = contract("tkb,kect->kbec", toks, mixed_back).astype(BF)
    g_ul, g_ll, g_ur, g_lr = ring_scatter(
        (
            grad_upper_left.reshape(in_left.shape),
            grad_lower_left.reshape(out_left.shape),
            grad_upper_right,
            grad_lower_right,
        ),
        2,
    )
    return ends[0], ends[1], g_ul, g_ur, g_lr, g_ll


def solution(mesh):
    in_specs = (
        P("dp", "block"),
        P("block", "dp", None),
        P("block", "dp", None),
        P("block", "dp", None),
        P("block", "dp", None),
        P("dp", "block"),
    )
    out_specs = (
        P("dp", "block"),
        P("dp", "block"),
        P("block", "dp", None),
        P("block", "dp", None),
        P("block", "dp", None),
        P("block", "dp", None),
    )
    return jax.shard_map(local, mesh=mesh, in_specs=in_specs, out_specs=out_specs, check_vma=False)
```

time: 941 us -> 279 us (0.30)
  waiting for transfers between devices: 801 us -> 20.5 us
  Pallas kernels: 0 us -> 133 us
  starting transfers between devices: 74.4 us -> 30.9 us
  blocking collectives: 0 us -> 33.7 us
  between operations: 14.3 us -> 1.04 us
  local copies, waits for them, and re-layouts: 20.6 us -> 30.2 us
    all_gather x4 -> x0, waiting for transfers between devices: 376 us -> none  [the longest x1 104 us: local(): lax.all_gather(upper_left, 'dp', axis=1, tiled=True)]
    reduce_scatter x4 -> x0, waiting for transfers between devices: 344 us -> none  [the longest x1 106 us: local(): lax.psum_scatter(grad_lower_right.astype(jnp.bfloat16), 'dp', scatter_dim...]
    pallas_call x0 -> x2, Pallas kernels: none -> 133 us  [the longest x1 70.8 us: ring_gather(): pl.pallas_call(functools.partial(gather_kernel, count), out_shape=shapes,...]
    all_to_all x4 -> x1, starting transfers between devices: 73.9 us -> 6.36 us  [exchange(): lax.all_to_all(values, 'block', split_axis=0, concat_axis=0, tiled=True,...]
    all_to_all x4 -> x1, waiting for transfers between devices: 77.6 us -> 20.5 us  [exchange(): lax.all_to_all(values, 'block', split_axis=0, concat_axis=0, tiled=True,...]
    all_to_all x0 -> x1, blocking collectives: none -> 33.7 us  [exchange(): lax.all_to_all(values, 'block', split_axis=0, concat_axis=0, tiled=True,...]
    ppermute x0 -> x2, starting transfers between devices: none -> 24.6 us  [local(): came = lax.ppermute(away, 'block', SWAP)]
    another operation x0 -> x8, local copies, waits for them, and re-layouts: none -> 16.8 us  [the longest x1 4.59 us: local(): left_four = in_left.reshape(ZH * kl, width, expand, width)]
  transfers between devices with their start and end apart: 12 -> 3, of which waited for: 11 -> 1; matrix products, arithmetic and copies ran while one was open for 4% -> 7% of each run, Pallas kernels for 0% -> 49%
where the time goes in v1:
time: 279 us; the launch traced here: 274 us
  Pallas kernels  133 us (48%)
  blocking collectives  33.7 us (12%)
  starting transfers between devices  30.9 us (11%)
  local copies, waits for them, and re-layouts  30.2 us (11%)
  waiting for transfers between devices  20.5 us (7%)
  matrix products  18.2 us (7%)
  other arithmetic  6.64 us (2%)
    pallas_call x1, Pallas kernels, ring_gather(): pl.pallas_call(functools.partial(gather_kernel, count), out_shape=shapes,...  70.8 us
    pallas_call x1, Pallas kernels, ring_scatter(): pl.pallas_call(functools.partial(scatter_kernel, count), out_shape=[jax.S...  62.4 us
    all_to_all x1, blocking collectives, exchange(): lax.all_to_all(values, 'block', split_axis=0, concat_axis=0, tiled=True,...  33.7 us
    ppermute x2, starting transfers between devices, local(): came = lax.ppermute(away, 'block', SWAP)  24.6 us
    all_to_all x1, waiting for transfers between devices, exchange(): lax.all_to_all(values, 'block', split_axis=0, concat_axis=0, tiled=True,...  20.5 us
    dot_general x12, matrix products, contract(): return jnp.einsum(form, left, right, preferred_element_type=F32)  18.2 us
    unnamed x42, local copies, waits for them, and re-layouts  7.9 us
    all_to_all x1, starting transfers between devices, exchange(): lax.all_to_all(values, 'block', split_axis=0, concat_axis=0, tiled=True,...  6.36 us
  transfers between devices with their start and end apart: 3, of which 1 were waited for; matrix products, arithmetic and copies ran while one was open for 7% of the time, Pallas kernels for 49%

profile of v1, /device:TPU:6, one launch (start us, length us, event | category | flops | bytes accessed | tf_op | source)
XLA Modules:
  0.0 274.4 jit_solution(11933637396780886631)
XLA Ops:
  0.7 1.1 fusion.21
  1.8 15.7 %collective-permute-start = (bf16[2,128,512]{2,1,0:T(8,128)(2,1)S(1)}, bf16[2,128,512]{2,1,0:T(8,128)(2,1)S(1)}, u32[]{:S(2)}, u32[]{:S(2)}) collective-permute-start(bf16[2,128,512]{2,1,0:T(8,128)(2,1)S(1)} %fusion.21), channel_id=1, source_target_pairs={{0,4},{1,5},{2,6},{3,7},{4,0},{5,1},{6,2},{7,3},{8,12},{9,13},{10,... | collective-permute-start | bytes 786440 | tf_op jit(solution)/shard_map/ppermute | solution.py:284
  17.5 70.8 %ring_gather.1 = (bf16[2,2,8,2,16,1024]{5,4,3,2,1,0:T(8,128)(2,1)}, bf16[2,2,8,2,64,256]{5,4,3,2,1,0:T(8,128)(2,1)}, bf16[2,8,8,2,16,256]{5,4,3,2,1,0:T(8,128)(2,1)}, bf16[2,8,8,2,16,256]{5,4,3,2,1,0:T(8,128)(2,1)}) custom-call(bf16[2,16,1024]{2,1,0:T(8,128)(2,1)} %refs_0_.1, bf16[2,64,256]{2,1,0:T(8,128)(2,1)} %refs_1_.1, bf16[8,16,256]{2,1,0:T(8,128)(2,1)} %refs_2_.1, ...), custom_call_target="tpu_custom_call" | custom-call | tf_op jit(solution)/shard_map/ring_gather/pallas_call | solution.py:120
  88.4 4.6 %reshape_reshape.13 = bf16[4,256,4,256]{3,2,1,0:T(4,128)(2,1)} reshape(bf16[2,2,8,2,16,1024]{5,4,3,2,1,0:T(8,128)(2,1)} %get-tuple-element.17) | data formatting | bytes 4194304 | tf_op jit(solution)/shard_map/reshape;reshape | solution.py:292
  93.5 1.2 copy-done
  95.4 1.2 copy.53
  96.6 0.9 fusion.11
  97.6 1.2 copy.52
  99.0 33.7 %all_to_all.10 = bf16[16,2,16,16,128]{4,3,2,1,0:T(8,128)(2,1)S(1)} all-to-all(bf16[16,2,16,16,128]{4,3,2,1,0:T(8,128)(2,1)S(1)} %bitcast.126), channel_id=1, replica_groups={{0,1,2,3,8,9,10,11,16,17,18,19,24,25,26,27},{4,5,6,7,12,13,14,15,20,21,..., dimensions={0} | all-to-all | bytes 4194304 | tf_op jit(solution)/shard_map/all_to_all | solution.py:244
  133.9 1.0 copy-done.10
  135.6 0.9 copy-done.9
  136.5 2.0 fusion.6
  138.6 1.3 convolution_convert_fusion.6
  140.9 1.2 copy.59
  142.1 1.2 copy.58
  143.3 1.6 pad_maximum_fusion.1
  144.9 6.4 %all-to-all-start.1 = ((bf16[16,2,16,16,128]{4,3,2,1,0:T(8,128)(2,1)}), bf16[16,2,16,16,128]{4,3,2,1,0:T(8,128)(2,1)S(1)}, u32[]{:S(2)}, u32[]{:S(2)}) async-start(bf16[16,2,16,16,128]{4,3,2,1,0:T(8,128)(2,1)} %bitcast.124), calls=%async_computation.1 | async-start | bytes 4194304 | tf_op jit(solution)/shard_map/all_to_all | solution.py:244
  151.3 3.7 %convolution_convert_fusion.1 = bf16[16,256,256]{2,1,0:T(8,128)(2,1)} fusion(bf16[16,256,128]{2,1,0:T(8,128)(2,1)} %bitcast.137, bf16[16,256,128]{2,1,0:T(8,128)(2,1)} %copy-done.3), kind=kOutput, calls=%fused_computation.13 | convolution fusion | flops 269484032 | bytes 4194304 | tf_op jit(solution)/shard_map/cat,cbt->cab/dot_general | solution.py:17
  155.0 2.3 convolution_convert_fusion
  157.3 20.5 %all-to-all-done.1 = bf16[16,2,16,16,128]{4,3,2,1,0:T(8,128)(2,1)S(1)} async-done(((bf16[16,2,16,16,128]{4,3,2,1,0:T(8,128)(2,1)}), bf16[16,2,16,16,128]{4,3,2,1,0:T(8,128)(2,1)S(1)}, u32[]{:S(2)}, u32[]{:S(2)}) %all-to-all-start.1) | async-done | bytes 2097184 | tf_op jit(solution)/shard_map/all_to_all | solution.py:244
  178.5 1.3 copy-done.8
  179.8 1.4 fusion.18
  182.8 1.6 fusion.17
  184.4 1.1 copy.64
  185.5 1.8 copy.65
  187.3 1.7 select_bitcast_fusion
  189.0 8.8 %collective-permute-start.1 = (bf16[2,128,512]{2,1,0:T(8,128)(2,1)}, bf16[2,128,512]{2,1,0:T(8,128)(2,1)}, u32[]{:S(2)}, u32[]{:S(2)}) collective-permute-start(bf16[2,128,512]{2,1,0:T(8,128)(2,1)} %select_bitcast_fusion), channel_id=1, source_target_pairs={{0,4},{1,5},{2,6},{3,7},{4,0},{5,1},{6,2},{7,3},{8,12},{9,13},{10,... | collective-permute-start | bytes 786440 | tf_op jit(solution)/shard_map/ppermute | solution.py:317
  197.8 3.0 %copy.66 = bf16[4,256,4,256]{3,2,1,0:T(4,128)(2,1)} copy(bf16[4,256,4,256]{3,1,2,0:T(8,128)(2,1)S(1)} %convolution_convert_fusion.3) | data formatting | bytes 4194304 | tf_op jit(solution)/shard_map/convert_element_type | solution.py:321
  200.8 4.5 %reshape_reshape.14.refs_0_ = bf16[2,2,8,2,16,1024]{5,4,3,2,1,0:T(8,128)(2,1)} reshape(bf16[4,256,4,256]{3,2,1,0:T(4,128)(2,1)} %copy.66) | data formatting | bytes 4194304 | tf_op jit(solution)/shard_map/reshape;reshape | solution.py:215
  205.3 2.1 convolution_convert_fusion.2
  207.4 62.4 %ring_scatter.1 = (f32[2,16,1024]{2,1,0:T(8,128)}, f32[2,64,256]{2,1,0:T(8,128)}, f32[8,16,256]{2,1,0:T(8,128)}, f32[8,16,256]{2,1,0:T(8,128)}) custom-call(bf16[2,2,8,2,16,1024]{5,4,3,2,1,0:T(8,128)(2,1)} %reshape_reshape.14.refs_0_, bf16[2,2,8,2,64,256]{5,4,3,2,1,0:T(8,128)(2,1)} %bitcast.130, bf16[2,8,8,2,16,256]{5,4,3,2,1,0:T(8,128)(2,1)} %bitcast.129, ...), custom_call_target="tpu_custom_call" | custom-call | tf_op jit(solution)/shard_map/ring_scatter/pallas_call | solution.py:216
  269.9 1.1 bitcast_select_fusion.2
  (56 shorter events, 10.0 us)
Async XLA Ops:
  1.8 91.2 %collective-permute-start = (bf16[2,128,512]{2,1,0:T(8,128)(2,1)S(1)}, bf16[2,128,512]{2,1,0:T(8,128)(2,1)S(1)}, u32[]{:S(2)}, u32[]{:S(2)}) collective-permute-start(bf16[2,128,512]{2,1,0:T(8,128)(2,1)S(1)} %fusion.21), channel_id=1, source_target_pairs={{0,4},{1,5},{2,6},{3,7},{4,0},{5,1},{6,2},{7,3},{8,12},{9,13},{10,... | collective-permute-start | bytes 786440 | tf_op jit(solution)/shard_map/ppermute | solution.py:284
  88.4 4.6 %copy-start.11 = (bf16[256,512]{1,0:T(8,128)(2,1)S(1)}, bf16[256,512]{1,0:T(8,128)(2,1)}, u32[]{:S(2)}) copy-start(bf16[256,512]{1,0:T(8,128)(2,1)} %param.11) | copy-start | bytes 786436
  88.4 4.6 %copy-start.12 = (bf16[256,512]{1,0:T(8,128)(2,1)S(1)}, bf16[256,512]{1,0:T(8,128)(2,1)}, u32[]{:S(2)}) copy-start(bf16[256,512]{1,0:T(8,128)(2,1)} %param.6) | copy-start | bytes 786436
  93.0 1.7 copy-start
  93.5 3.1 %copy-start.5 = (bf16[1,128,2,512]{1,3,2,0:T(8,128)(2,1)}, bf16[1,128,2,512]{1,3,2,0:T(8,128)(2,1)S(1)}, u32[]{:S(2)}) copy-start(bf16[1,128,2,512]{1,3,2,0:T(8,128)(2,1)S(1)} %copy.50) | copy-start | bytes 786436
  94.7 2.0 copy-start.7
  133.3 1.6 copy-start.10
  133.9 1.7 copy-start.2
  134.9 1.6 copy-start.9
  138.5 1.4 copy-start.17
  138.5 1.6 copy-start.3
  144.9 32.9 %all-to-all-start.1 = ((bf16[16,2,16,16,128]{4,3,2,1,0:T(8,128)(2,1)}), bf16[16,2,16,16,128]{4,3,2,1,0:T(8,128)(2,1)S(1)}, u32[]{:S(2)}, u32[]{:S(2)}) async-start(bf16[16,2,16,16,128]{4,3,2,1,0:T(8,128)(2,1)} %bitcast.124), calls=%async_computation.1 | async-start | bytes 4194304 | tf_op jit(solution)/shard_map/all_to_all | solution.py:244
  151.3 3.8 %copy-start.18 = (f32[16,256,128]{2,1,0:T(8,128)S(1)}, f32[16,256,128]{2,1,0:T(8,128)}, u32[]{:S(2)}) copy-start(f32[16,256,128]{2,1,0:T(8,128)} %copy-done.17) | copy-start | bytes 6291460
  178.2 1.6 copy-start.8
  181.2 1.6 copy-start.1
  189.0 80.9 %collective-permute-start.1 = (bf16[2,128,512]{2,1,0:T(8,128)(2,1)}, bf16[2,128,512]{2,1,0:T(8,128)(2,1)}, u32[]{:S(2)}, u32[]{:S(2)}) collective-permute-start(bf16[2,128,512]{2,1,0:T(8,128)(2,1)} %select_bitcast_fusion), channel_id=1, source_target_pairs={{0,4},{1,5},{2,6},{3,7},{4,0},{5,1},{6,2},{7,3},{8,12},{9,13},{10,... | collective-permute-start | bytes 786440 | tf_op jit(solution)/shard_map/ppermute | solution.py:317
  200.8 4.5 %copy-start.6 = (bf16[1,128,2,512]{1,3,2,0:T(8,128)(2,1)S(1)}, bf16[1,128,2,512]{1,3,2,0:T(8,128)(2,1)}, u32[]{:S(2)}) copy-start(bf16[1,128,2,512]{1,3,2,0:T(8,128)(2,1)} %copy-done.5) | copy-start | bytes 786436
  207.4 62.4 %copy-start.4 = (bf16[1,128,2,512]{3,1,0,2:T(8,128)(2,1)S(1)}, bf16[1,128,2,512]{3,1,0,2:T(8,128)(2,1)}, u32[]{:S(2)}) copy-start(bf16[1,128,2,512]{3,1,0,2:T(8,128)(2,1)} %copy.65) | copy-start | bytes 786436
  269.8 2.0 copy-start.16
  269.8 2.6 copy-start.15
  269.8 3.3 %copy-start.14 = (f32[8,16,256]{2,1,0:T(8,128)S(1)}, f32[8,16,256]{2,1,0:T(8,128)}, u32[]{:S(2)}) copy-start(f32[8,16,256]{2,1,0:T(8,128)} %get-tuple-element.52) | copy-start | bytes 393220
  269.8 3.9 %copy-start.13 = (f32[2,64,256]{2,1,0:T(8,128)S(1)}, f32[2,64,256]{2,1,0:T(8,128)}, u32[]{:S(2)}) copy-start(f32[2,64,256]{2,1,0:T(8,128)} %get-tuple-element.53) | copy-start | bytes 393220

commit v2 on v1

v2 whole, which is shorter than its diff:
```python
import functools

import jax
import jax.numpy as jnp
from jax import lax
from jax.experimental import pallas as pl
from jax.experimental.pallas import tpu as pltpu
from jax.sharding import PartitionSpec as P

ZL, CORES, NY, ZH, NX = 8, 2, 4, 2, 4
RING = ZL * ZH
BF = jnp.bfloat16
F32 = jnp.float32


def contract(form, left, right):
    return jnp.einsum(form, left, right, preferred_element_type=F32)


def place():
    dp = lax.axis_index("dp")
    block = lax.axis_index("block")
    zl, core = dp // CORES, dp % CORES
    y, rest = block // (ZH * NX), block % (ZH * NX)
    zh, x = rest // NX, rest % NX
    return zl, core, y, zh, x


def at(z, core, y, x):
    z = z % RING
    return {
        "dp": (z % ZL) * CORES + core,
        "block": y * (ZH * NX) + (z // ZL) * NX + x,
    }


def greet(others):
    barrier = pltpu.get_barrier_semaphore()
    for who in others:
        pl.semaphore_signal(barrier, inc=1, device_id=who, device_id_type=pl.DeviceIdType.MESH)
    pl.semaphore_wait(barrier, len(others))


def remote(src, dst, send, recv, target):
    return pltpu.make_async_remote_copy(
        src_ref=src,
        dst_ref=dst,
        send_sem=send,
        recv_sem=recv,
        device_id=target,
        device_id_type=pl.DeviceIdType.MESH,
    )


class Swap:
    STEPS = (3,)
    WAYS = (RING // 4, RING - RING // 4)

    @staticmethod
    def scratch(arrays):
        shape = arrays[0].shape
        return [
            pltpu.VMEM(shape, BF),
            pltpu.SemaphoreType.DMA((2, 2)),
            pltpu.SemaphoreType.DMA((2, 2)),
        ]

    @staticmethod
    def outs(arrays):
        return [jax.ShapeDtypeStruct(v.shape, v.dtype) for v in arrays]

    def __init__(self, ins, outs, scratch):
        self.src, self.out = ins[0], outs[0]
        self.relay, self.send, self.recv = scratch
        zl, core, y, zh, x = place()
        z = zh * ZL + zl
        self.targets = [at(z + way, core, y, x) for way in self.WAYS]

    def peers(self):
        return self.targets

    def start(self):
        self.first = [
            remote(
                self.src.at[j], self.relay.at[j], self.send.at[0, j], self.recv.at[0, j], who
            )
            for j, who in enumerate(self.targets)
        ]
        for copy in self.first:
            copy.start()

    def step(self, s):
        if s not in self.STEPS:
            return
        self.second = []
        for j, who in enumerate(self.targets):
            self.first[j].wait_recv()
            copy = remote(
                self.relay.at[j], self.out.at[j], self.send.at[1, j], self.recv.at[1, j], who
            )
            copy.start()
            self.second.append(copy)

    def finish(self):
        for copy in self.second:
            copy.wait_recv()
        for copy in self.first + self.second:
            copy.wait_send()


class Spread:
    RELAYS = (
        (0, 2, 0, 1),
        (2, 0, 1, 0),
        (3, 2, 0, 3),
        (2, 1, 3, 0),
        (1, 2, 0, 1),
        (2, 3, 3, 0),
        (2, 2, 0, 3),
    )
    STEPS = {3: (0, 1, 2), 5: (3, 4, 5, 6)}

    @staticmethod
    def scratch(arrays):
        n, hops = len(arrays), len(Spread.RELAYS)
        return [pltpu.VMEM((hops,) + v.shape[1:], BF) for v in arrays] + [
            pltpu.SemaphoreType.DMA((n, NY * NX)),
            pltpu.SemaphoreType.DMA((n, NY * NX)),
            pltpu.SemaphoreType.DMA((n, hops)),
            pltpu.SemaphoreType.DMA((n, hops)),
            pltpu.SemaphoreType.DMA((n,)),
        ]

    @staticmethod
    def outs(arrays):
        return [jax.ShapeDtypeStruct(v.shape, v.dtype) for v in arrays]

    def __init__(self, ins, outs, scratch):
        self.n = len(ins)
        self.src, self.out = ins, outs
        self.relay = scratch[: self.n]
        self.send, self.recv, self.rsend, self.rrecv, self.own = scratch[self.n :]
        zl, self.core, self.y, zh, self.x = place()
        self.z = zh * ZL + zl

    def device(self, dy, dx):
        return at(self.z, self.core, (self.y + dy) % NY, (self.x + dx) % NX)

    def index(self, dy, dx):
        return (self.y + dy) % NY * NX + (self.x + dx) % NX

    def peers(self):
        return [self.device(dy, dx) for dy in range(NY) for dx in range(NX) if dy or dx]

    def start(self):
        me = self.index(0, 0)
        self.sent, self.legs, self.keeps, self.comes = [], {}, [], []
        for j, (dy, dx, ry, rx) in enumerate(self.RELAYS):
            for w in range(self.n):
                copy = remote(
                    self.src[w].at[self.index(dy, dx)],
                    self.relay[w].at[j],
                    self.rsend.at[w, j],
                    self.rrecv.at[w, j],
                    self.device(ry, rx),
                )
                copy.start()
                self.legs[w, j] = copy
        for dy in range(NY):
            for dx in range(NX):
                if not (dy or dx) or 2 in (dy, dx):
                    continue
                for w in range(self.n):
                    copy = remote(
                        self.src[w].at[self.index(dy, dx)],
                        self.out[w].at[me],
                        self.send.at[w, dy * NX + dx],
                        self.recv.at[w, dy * NX + dx],
                        self.device(dy, dx),
                    )
                    copy.start()
                    self.sent.append(copy)
                    self.comes.append(copy)
        for w in range(self.n):
            keep = pltpu.make_async_copy(self.src[w].at[me], self.out[w].at[me], self.own.at[w])
            keep.start()
            self.keeps.append(keep)

    def step(self, s):
        for j in self.STEPS.get(s, ()):
            dy, dx, ry, rx = self.RELAYS[j]
            for w in range(self.n):
                self.legs[w, j].wait_recv()
                self.sent.append(self.legs[w, j])
                copy = remote(
                    self.relay[w].at[j],
                    self.out[w].at[self.index(NY - ry, NX - rx)],
                    self.send.at[w, dy * NX + dx],
                    self.recv.at[w, dy * NX + dx],
                    self.device(dy - ry + NY, dx - rx + NX),
                )
                copy.start()
                self.sent.append(copy)
                self.comes.append(copy)

    def finish(self):
        for copy in self.comes:
            copy.wait_recv()
        for copy in self.sent:
            copy.wait_send()
        for keep in self.keeps:
            keep.wait()


def gather_kernel(count, kind, extra, *refs):
    own, refs = refs[:count], refs[count:]
    side_in, refs = refs[:extra], refs[extra:]
    out, refs = refs[:count], refs[count:]
    side_out, refs = refs[:extra], refs[extra:]
    (send, recv, local), refs = refs[:3], refs[3:]
    side = kind(side_in, side_out, refs)
    zl, core, y, zh, x = place()
    z = zh * ZL + zl
    right, left = at(z + 1, core, y, x), at(z + RING - 1, core, y, x)
    other = at(z, 1 - core, y, x)
    greet([right, left, other] + side.peers())

    def spot(w, source):
        source = source % RING
        return out[w].at[source // ZL, :, source % ZL, core]

    def push(w, slot, source, target, src=None):
        where = spot(w, source)
        copy = remote(
            where if src is None else src, where, send.at[w, slot], recv.at[w, slot], target
        )
        copy.start()
        return copy

    half = RING // 2
    sent = []
    rights, lefts, keeps = [], [], []
    for w in range(count):
        src = own[w]
        rights.append(push(w, 0, z, right, src))
        lefts.append(push(w, half, z, left, src))
    side.start()
    for w in range(count):
        src = own[w]
        sent.append(push(w, RING - 1, z, other, src))
        keep = pltpu.make_async_copy(src, spot(w, z), local.at[w])
        keep.start()
        keeps.append(keep)
    for s in range(1, half + 1):
        for w in range(count):
            rights[w].wait_recv()
            sent.append(rights[w])
            if s < half:
                rights[w] = push(w, s, z + RING - s, right)
            sent.append(push(w, RING + s, z + RING - s, other))
            if s < half:
                lefts[w].wait_recv()
                sent.append(lefts[w])
                if s < half - 1:
                    lefts[w] = push(w, half + s, z + s, left)
                sent.append(push(w, RING + half + s, z + s, other))
        side.step(s)
    side.finish()
    for w in range(count):
        for slot in [RING - 1] + list(range(RING + 1, 2 * RING)):
            remote(own[w], own[w], send.at[w, slot], recv.at[w, slot], other).wait_recv()
    for copy in sent:
        copy.wait_send()
    for keep in keeps:
        keep.wait()


def ring_gather(shards, kind, arrays, collective_id):
    count, extra = len(shards), len(arrays)
    slots = 2 * RING
    shapes = [
        jax.ShapeDtypeStruct((ZH, s.shape[0], ZL, CORES) + s.shape[1:], s.dtype) for s in shards
    ]
    outs = pl.pallas_call(
        functools.partial(gather_kernel, count, kind, extra),
        out_shape=shapes + kind.outs(arrays),
        in_specs=[pl.BlockSpec(memory_space=pltpu.VMEM)] * (count + extra),
        out_specs=[pl.BlockSpec(memory_space=pl.ANY)] * (count + extra),
        scratch_shapes=[
            pltpu.SemaphoreType.DMA((count, slots)),
            pltpu.SemaphoreType.DMA((count, slots)),
            pltpu.SemaphoreType.DMA((count,)),
        ]
        + kind.scratch(arrays),
        compiler_params=pltpu.CompilerParams(collective_id=collective_id, has_side_effects=True),
        name="ring_gather",
    )(*shards, *arrays)
    full = [
        o.reshape(ZH * s.shape[0], ZL * CORES * s.shape[1], s.shape[2])
        for o, s in zip(outs[:count], shards)
    ]
    return full, outs[count:]


def scatter_kernel(count, kind, extra, *refs):
    part, refs = refs[:count], refs[count:]
    side_in, refs = refs[:extra], refs[extra:]
    out, refs = refs[:count], refs[count:]
    side_out, refs = refs[:extra], refs[extra:]
    mate, come, stage = refs[:count], refs[count : 2 * count], refs[2 * count : 3 * count]
    (send, recv, msend, mrecv), refs = refs[3 * count : 3 * count + 4], refs[3 * count + 4 :]
    side = kind(side_in, side_out, refs)
    zl, core, y, zh, x = place()
    z = zh * ZL + zl
    right, left = at(z + 1, core, y, x), at(z + RING - 1, core, y, x)
    other = at(z, 1 - core, y, x)
    greet([right, left, other] + side.peers())
    half = RING // 2

    def goal(slot):
        if slot < half:
            return (z + half - slot) % RING
        return (z + RING - (half - 1) + (slot - half)) % RING

    order = []
    for s in range(half):
        order.append(s)
        if half + s < RING - 1:
            order.append(half + s)
    order.append(RING - 1)

    mates = {}

    def trade(slot):
        d = goal(slot)
        for w in range(count):
            copy = remote(
                part[w].at[d // ZL, :, d % ZL, 1 - core],
                mate[w].at[slot],
                msend.at[w, slot],
                mrecv.at[w, slot],
                other,
            )
            copy.start()
            mates[w, slot] = copy

    for slot in order[:4]:
        trade(slot)
    side.start()
    for slot in order[4:]:
        trade(slot)
    moves = {}
    for slot in order:
        d = goal(slot)
        for w in range(count):
            mates[w, slot].wait_recv()
            total = part[w][d // ZL, :, d % ZL, core].astype(F32) + mate[w][slot].astype(F32)
            if slot == RING - 1:
                for last in (half - 1, RING - 2):
                    moves[w, last].wait_recv()
                    total = total + come[w][last].astype(F32)
                out[w][...] = total
                continue
            if slot not in (0, half):
                moves[w, slot - 1].wait_recv()
                total = total + come[w][slot - 1].astype(F32)
            stage[w][slot] = total.astype(BF)
            copy = remote(
                stage[w].at[slot],
                come[w].at[slot],
                send.at[w, slot],
                recv.at[w, slot],
                right if slot < half else left,
            )
            copy.start()
            moves[w, slot] = copy
        if slot < half:
            side.step(slot)
    side.finish()
    for copy in mates.values():
        copy.wait_send()
    for copy in moves.values():
        copy.wait_send()


def ring_scatter(parts, kind, arrays, collective_id):
    count, extra = len(parts), len(arrays)
    split, shards = [], []
    for p in parts:
        shard = (p.shape[0] // ZH, p.shape[1] // (ZL * CORES), p.shape[2])
        shards.append(shard)
        split.append(p.reshape(ZH, shard[0], ZL, CORES, shard[1], shard[2]))
    outs = pl.pallas_call(
        functools.partial(scatter_kernel, count, kind, extra),
        out_shape=[jax.ShapeDtypeStruct(s, F32) for s in shards] + kind.outs(arrays),
        in_specs=[pl.BlockSpec(memory_space=pltpu.VMEM)] * (count + extra),
        out_specs=[pl.BlockSpec(memory_space=pltpu.VMEM)] * count
        + [pl.BlockSpec(memory_space=pl.ANY)] * extra,
        scratch_shapes=[pltpu.VMEM((RING,) + s, BF) for s in shards]
        + [pltpu.VMEM((RING - 1,) + s, BF) for s in shards]
        + [pltpu.VMEM((RING - 1,) + s, BF) for s in shards]
        + [
            pltpu.SemaphoreType.DMA((count, RING - 1)),
            pltpu.SemaphoreType.DMA((count, RING - 1)),
            pltpu.SemaphoreType.DMA((count, RING)),
            pltpu.SemaphoreType.DMA((count, RING)),
        ]
        + kind.scratch(arrays),
        compiler_params=pltpu.CompilerParams(
            collective_id=collective_id, has_side_effects=True, vmem_limit_bytes=48 * 2**20
        ),
        name="ring_scatter",
    )(*split, *arrays)
    return outs[:count], outs[count:]


def columns_out(v):
    k, e, c, t = v.shape
    cols = c // (NY * ZH * NX)
    v = v.reshape(k * e, NY, ZH, NX, cols, t).transpose(1, 3, 2, 4, 0, 5)
    return v.reshape(NY * NX, ZH * cols, k * e, t)


def columns_in(v):
    peers, c, a, t = v.shape
    v = v.reshape(NY, NX, c, ZH, a // ZH, t).transpose(2, 0, 3, 1, 4, 5)
    return v.reshape(c, peers * a, t)


def rows_out(v):
    c, a, t = v.shape
    rows = a // (NY * ZH * NX)
    v = v.reshape(c, NY, ZH, NX, rows, t).transpose(1, 3, 2, 4, 0, 5)
    return v.reshape(NY * NX, ZH * rows, c, t)


def rows_in(v, k):
    peers, a, c, t = v.shape
    v = v.reshape(NY, NX, a, ZH, c // ZH, t).transpose(2, 0, 3, 1, 4, 5)
    return v.reshape(k, a // k * peers * c, t)


def local(tokens, upper_left, upper_right, lower_right, lower_left, cotangent):
    zl, core, y, zh, x = place()
    rows, features = tokens.shape
    width = upper_left.shape[1] * ZL * CORES
    kl = upper_left.shape[0]
    k4 = ZH * kl
    expand = upper_left.shape[2] // width
    few = rows // ZH
    low = zh == 0

    both = jnp.stack([tokens, cotangent]).reshape(2, ZH, few, kl, width).transpose(0, 1, 3, 2, 4)
    mine = jnp.where(low, both[:, 0], both[:, 1])
    away = jnp.where(low, both[:, 1], both[:, 0])
    (in_left, out_left), (came,) = ring_gather((upper_left, lower_left), Swap, (away,), 1)
    pair = jnp.concatenate(
        [jnp.where(low, mine, came), jnp.where(low, came, mine)], axis=1
    )
    toks, cots = pair[0], pair[1]

    mixed = contract("ktb,kbj->kjt", toks, in_left).astype(BF)
    back_narrow = contract("kto,kjo->kjt", cots, out_left).astype(BF)
    (in_right, out_right), (spread, narrow_back) = ring_gather(
        (upper_right, lower_right),
        Spread,
        (
            columns_out(mixed.reshape(k4, expand, width, few)),
            columns_out(back_narrow.reshape(k4, expand, width, few)),
        ),
        2,
    )
    spread, narrow_back = columns_in(spread), columns_in(narrow_back)

    hidden_pre = contract("cat,cab->cbt", spread, in_right)
    active = jax.nn.gelu(hidden_pre).astype(BF)
    narrow = contract("cbt,cbe->cet", active, out_right).astype(BF)
    back_active = contract("cet,cbe->cbt", narrow_back, out_right)
    back_pre = jax.vjp(jax.nn.gelu, hidden_pre)[1](back_active)[0].astype(BF)
    back_mixed = contract("cbt,cab->cat", back_pre, in_right).astype(BF)
    grad_lower_right = contract("cbt,cet->cbe", active, narrow_back).astype(BF)
    grad_upper_right = contract("cat,cbt->cab", spread, back_pre).astype(BF)
    (g_ur, g_lr), (narrow, back_mixed) = ring_scatter(
        (grad_upper_right, grad_lower_right), Spread, (rows_out(narrow), rows_out(back_mixed)), 3
    )
    narrow, back_mixed = rows_in(narrow, k4), rows_in(back_mixed, k4)

    result = contract("kjt,kjo->kto", narrow, out_left).astype(BF)
    token_grad = contract("kjt,kbj->ktb", back_mixed, in_left).astype(BF)
    grad_lower_left = contract("kjt,kto->kjo", narrow, cots).astype(BF)
    grad_upper_left = contract("ktb,kjt->kbj", toks, back_mixed).astype(BF)

    ends = jnp.stack([result, token_grad]).reshape(2, ZH, kl, few, width)
    keep = jnp.where(low, ends[:, 0], ends[:, 1])
    away = jnp.where(low, ends[:, 1], ends[:, 0])
    (g_ul, g_ll), (came,) = ring_scatter((grad_upper_left, grad_lower_left), Swap, (away,), 4)
    ends = jnp.stack([jnp.where(low, keep, came), jnp.where(low, came, keep)], axis=1)
    ends = ends.transpose(0, 1, 3, 2, 4).reshape(2, rows, features)
    return ends[0], ends[1], g_ul, g_ur, g_lr, g_ll


def solution(mesh):
    in_specs = (
        P("dp", "block"),
        P("block", "dp", None),
        P("block", "dp", None),
        P("block", "dp", None),
        P("block", "dp", None),
        P("dp", "block"),
    )
    out_specs = (
        P("dp", "block"),
        P("dp", "block"),
        P("block", "dp", None),
        P("block", "dp", None),
        P("block", "dp", None),
        P("block", "dp", None),
    )
    return jax.shard_map(local, mesh=mesh, in_specs=in_specs, out_specs=out_specs, check_vma=False)
```

time: 279 us -> 246 us (0.88)
  Pallas kernels: 133 us -> 208 us
  blocking collectives: 33.7 us -> 0 us
  starting transfers between devices: 30.9 us -> 0 us
  waiting for transfers between devices: 20.5 us -> 0 us
  local copies, waits for them, and re-layouts: 30.2 us -> 18.6 us
  other arithmetic: 6.64 us -> 1.94 us
  matrix products: 18.2 us -> 15.1 us
    pallas_call x2 -> x4, Pallas kernels: 133 us -> 208 us  [the longest x2 111 us: ring_gather(): pl.pallas_call(functools.partial(gather_kernel, count, kind, extra), out_...]
    all_to_all x1 -> x0, blocking collectives: 33.7 us -> none  [exchange(): lax.all_to_all(values, 'block', split_axis=0, concat_axis=0, tiled=True,...]
    ppermute x2 -> x0, starting transfers between devices: 24.6 us -> none  [local(): came = lax.ppermute(away, 'block', SWAP)]
    all_to_all x1 -> x0, waiting for transfers between devices: 20.5 us -> none  [exchange(): lax.all_to_all(values, 'block', split_axis=0, concat_axis=0, tiled=True,...]
    another operation x8 -> x6, local copies, waits for them, and re-layouts: 16.8 us -> 6.53 us  [the longest x2 4.44 us: columns_out(): v = v.reshape(k * e, NY, ZH, NX, cols, t).transpose(1, 3, 2, 4, 0, 5)]
    all_to_all x1 -> x0, starting transfers between devices: 6.36 us -> none  [exchange(): lax.all_to_all(values, 'block', split_axis=0, concat_axis=0, tiled=True,...]
    dot_general x12, matrix products: 18.2 us -> 15.1 us  [contract(): return jnp.einsum(form, left, right, preferred_element_type=F32)]
    convert_element_type x1 -> x0, local copies, waits for them, and re-layouts: 2.99 us -> none  [local(): grad_upper_left = contract('tkb,kect->kbec', toks, mixed_back).astype(BF)]
  transfers between devices with their start and end apart: 3 -> 0, of which waited for: 1 -> 0; matrix products, arithmetic and copies ran while one was open for 7% -> 0% of each run, Pallas kernels for 49% -> 0%
where the time goes in v2:
time: 246 us; the launch traced here: 244 us
  Pallas kernels  208 us (85%)
  local copies, waits for them, and re-layouts  18.6 us (8%)
  matrix products  15.1 us (6%)
    pallas_call x2, Pallas kernels, ring_gather(): pl.pallas_call(functools.partial(gather_kernel, count, kind, extra), out_...  111 us
    pallas_call x2, Pallas kernels, ring_scatter(): pl.pallas_call(functools.partial(scatter_kernel, count, kind, extra), out...  96.2 us
    dot_general x12, matrix products, contract(): return jnp.einsum(form, left, right, preferred_element_type=F32)  15.1 us
    unnamed x16, local copies, waits for them, and re-layouts  6.51 us

profile of v2, /device:TPU:6, one launch (start us, length us, event | category | flops | bytes accessed | tf_op | source)
XLA Modules:
  0.0 244.2 jit_solution(6065377083116070860)
XLA Ops:
  0.7 1.0 stack.27
  1.7 1.0 stack.28
  2.8 0.7 select_bitcast_fusion.1.refs_2_
  3.6 68.6 %ring_gather.2 = (bf16[2,2,8,2,16,1024]{5,4,3,2,1,0:T(8,128)(2,1)}, bf16[2,2,8,2,64,256]{5,4,3,2,1,0:T(8,128)(2,1)}, bf16[2,2,128,256]{3,2,1,0:T(8,128)(2,1)}) custom-call(bf16[2,16,1024]{2,1,0:T(8,128)(2,1)} %refs_0_.2, bf16[2,64,256]{2,1,0:T(8,128)(2,1)} %refs_1_.2, bf16[2,2,128,256]{3,2,1,0:T(8,128)(2,1)} %select_bitcast_fusion.1.refs_2_), custom_call_target="tpu_custom_call" | custom-call | tf_op jit(solution)/shard_map/ring_gather/pallas_call | solution.py:284
  72.2 1.0 bitcast_select_fusion.2
  73.2 2.4 %convolution_convert_fusion.4 = bf16[4,1024,128]{2,1,0:T(8,128)(2,1)S(1)} fusion(bf16[4,1024,256]{2,1,0:T(8,128)(2,1)} %bitcast.109, bf16[2,2,128,256]{3,2,1,0:T(8,128)(2,1)S(1)} %get-tuple-element.36, bf16[2,2,128,256]{3,2,1,0:T(8,128)(2,1)S(1)} %get-tuple-element.37), kind=kOutput, calls=%fused_computation.14 | convolution fusion | flops 269090816 | bytes 3670016 | tf_op jit(solution)/shard_map/kto,kjo->kjt/dot_general | solution.py:17
  75.7 2.2 copy.30
  77.9 0.9 convolution_convert_fusion.5
  78.8 2.2 copy.29
  81.0 42.8 %ring_gather.3 = (bf16[2,8,8,2,16,256]{5,4,3,2,1,0:T(8,128)(2,1)}, bf16[2,8,8,2,16,256]{5,4,3,2,1,0:T(8,128)(2,1)}, bf16[16,16,16,128]{3,2,1,0:T(8,128)(2,1)}, bf16[16,16,16,128]{3,2,1,0:T(8,128)(2,1)}) custom-call(bf16[8,16,256]{2,1,0:T(8,128)(2,1)} %refs_0_.3, bf16[8,16,256]{2,1,0:T(8,128)(2,1)} %refs_1_.3, bf16[16,16,16,128]{3,2,1,0:T(8,128)(2,1)} %bitcast.116, ...), custom_call_target="tpu_custom_call" | custom-call | tf_op jit(solution)/shard_map/ring_gather/pallas_call | solution.py:284
  123.8 1.7 copy.31
  126.1 0.7 fusion.20
  126.8 0.9 copy-done.2
  127.7 2.0 fusion.6
  129.7 1.3 convolution_convert_fusion.7
  131.0 0.7 convolution_convert_fusion.6
  131.7 2.0 convolution_convert_fusion.3
  133.7 1.2 copy.36
  134.9 1.2 copy.35
  136.2 2.2 convolution_convert_fusion.2
  138.4 40.9 %ring_scatter.2 = (f32[8,16,256]{2,1,0:T(8,128)S(1)}, f32[8,16,256]{2,1,0:T(8,128)S(1)}, bf16[16,16,16,128]{3,2,1,0:T(8,128)(2,1)S(1)}, bf16[16,16,16,128]{3,2,1,0:T(8,128)(2,1)S(1)}) custom-call(bf16[2,8,8,2,16,256]{5,4,3,2,1,0:T(8,128)(2,1)} %bitcast.106, bf16[2,8,8,2,16,256]{5,4,3,2,1,0:T(8,128)(2,1)} %bitcast.124, ...), custom_call_target="tpu_custom_call" | custom-call | tf_op jit(solution)/shard_map/ring_scatter/pallas_call | solution.py:393
  179.6 1.3 copy-done.1
  181.7 0.8 convolution_convert_fusion.8
  182.6 0.8 convolution_convert_fusion.1
  183.4 0.7 convolution_convert_fusion
  184.1 55.3 %ring_scatter.3 = (f32[2,16,1024]{2,1,0:T(8,128)S(1)}, f32[2,64,256]{2,1,0:T(8,128)S(1)}, bf16[2,2,128,256]{3,2,1,0:T(8,128)(2,1)S(1)}) custom-call(bf16[2,2,8,2,16,1024]{5,4,3,2,1,0:T(8,128)(2,1)S(1)} %bitcast.96, bf16[2,2,8,2,64,256]{5,4,3,2,1,0:T(8,128)(2,1)S(1)} %bitcast.97, bf16[2,2,128,256]{3,2,1,0:T(8,128)(2,1)S(1)} %select_bitcast_fusion.refs_2_), custom_call_target="tpu_custom_call" | custom-call | tf_op jit(solution)/shard_map/ring_scatter/pallas_call | solution.py:393
  239.8 0.7 copy.51
  240.8 0.7 copy.50
  241.6 0.7 copy.56
  242.2 0.7 copy.57
  242.9 0.7 copy.58
  243.5 0.7 copy.59
  (21 shorter events, 2.5 us)
Async XLA Ops:
  73.2 4.7 %copy-start = (bf16[2,2,8,2,16,1024]{5,4,3,2,1,0:T(8,128)(2,1)S(1)}, bf16[2,2,8,2,16,1024]{5,4,3,2,1,0:T(8,128)(2,1)}, u32[]{:S(2)}) copy-start(bf16[2,2,8,2,16,1024]{5,4,3,2,1,0:T(8,128)(2,1)} %get-tuple-element.20) | copy-start | bytes 6291460
  123.8 1.7 copy-start.4
  123.8 2.2 copy-start.3
  126.1 1.6 copy-start.2
  179.3 1.6 copy-start.1

commit v3 on v2

--- a/solution.py
+++ b/solution.py
@@ -11,6 +11,7 @@
 RING = ZL * ZH
 BF = jnp.bfloat16
 F32 = jnp.float32
+PIECES = 2
 
 
 def contract(form, left, right):
@@ -118,7 +119,7 @@
         (2, 3, 3, 0),
         (2, 2, 0, 3),
     )
-    STEPS = {3: (0, 1, 2), 5: (3, 4, 5, 6)}
+    STEPS = {1: (0, 1, 2), 2: (3, 4, 5, 6)}
 
     @staticmethod
     def scratch(arrays):
@@ -212,6 +213,14 @@
             keep.wait()
 
 
+def halves(shapes):
+    return [
+        (w, pl.ds(i * (s[0] // PIECES), s[0] // PIECES))
+        for w, s in enumerate(shapes)
+        for i in range(PIECES)
+    ]
+
+
 def gather_kernel(count, kind, extra, *refs):
     own, refs = refs[:count], refs[count:]
     side_in, refs = refs[:extra], refs[extra:]
@@ -225,14 +234,22 @@
     other = at(z, 1 - core, y, x)
     greet([right, left, other] + side.peers())
 
-    def spot(w, source):
+    pieces = halves([o.shape for o in own])
+    total = range(len(pieces))
+
+    def mine(p):
+        w, part = pieces[p]
+        return own[w].at[part]
+
+    def spot(p, source):
+        w, part = pieces[p]
         source = source % RING
-        return out[w].at[source // ZL, :, source % ZL, core]
-
-    def push(w, slot, source, target, src=None):
-        where = spot(w, source)
+        return out[w].at[source // ZL, part, source % ZL, core]
+
+    def push(p, slot, source, target, src=None):
+        where = spot(p, source)
         copy = remote(
-            where if src is None else src, where, send.at[w, slot], recv.at[w, slot], target
+            where if src is None else src, where, send.at[p, slot], recv.at[p, slot], target
         )
         copy.start()
         return copy
@@ -240,35 +257,33 @@
     half = RING // 2
     sent = []
     rights, lefts, keeps = [], [], []
-    for w in range(count):
-        src = own[w]
-        rights.append(push(w, 0, z, right, src))
-        lefts.append(push(w, half, z, left, src))
+    for p in total:
+        rights.append(push(p, 0, z, right, mine(p)))
+        lefts.append(push(p, half, z, left, mine(p)))
     side.start()
-    for w in range(count):
-        src = own[w]
-        sent.append(push(w, RING - 1, z, other, src))
-        keep = pltpu.make_async_copy(src, spot(w, z), local.at[w])
+    for p in total:
+        sent.append(push(p, RING - 1, z, other, mine(p)))
+        keep = pltpu.make_async_copy(mine(p), spot(p, z), local.at[p])
         keep.start()
         keeps.append(keep)
     for s in range(1, half + 1):
-        for w in range(count):
-            rights[w].wait_recv()
-            sent.append(rights[w])
+        for p in total:
+            rights[p].wait_recv()
+            sent.append(rights[p])
             if s < half:
-                rights[w] = push(w, s, z + RING - s, right)
-            sent.append(push(w, RING + s, z + RING - s, other))
+                rights[p] = push(p, s, z + RING - s, right)
+            sent.append(push(p, RING + s, z + RING - s, other))
             if s < half:
-                lefts[w].wait_recv()
-                sent.append(lefts[w])
+                lefts[p].wait_recv()
+                sent.append(lefts[p])
                 if s < half - 1:
-                    lefts[w] = push(w, half + s, z + s, left)
-                sent.append(push(w, RING + half + s, z + s, other))
+                    lefts[p] = push(p, half + s, z + s, left)
+                sent.append(push(p, RING + half + s, z + s, other))
         side.step(s)
     side.finish()
-    for w in range(count):
+    for p in total:
         for slot in [RING - 1] + list(range(RING + 1, 2 * RING)):
-            remote(own[w], own[w], send.at[w, slot], recv.at[w, slot], other).wait_recv()
+            remote(mine(p), mine(p), send.at[p, slot], recv.at[p, slot], other).wait_recv()
     for copy in sent:
         copy.wait_send()
     for keep in keeps:
@@ -287,12 +302,14 @@
         in_specs=[pl.BlockSpec(memory_space=pltpu.VMEM)] * (count + extra),
         out_specs=[pl.BlockSpec(memory_space=pl.ANY)] * (count + extra),
         scratch_shapes=[
-            pltpu.SemaphoreType.DMA((count, slots)),
-            pltpu.SemaphoreType.DMA((count, slots)),
-            pltpu.SemaphoreType.DMA((count,)),
+            pltpu.SemaphoreType.DMA((count * PIECES, slots)),
+            pltpu.SemaphoreType.DMA((count * PIECES, slots)),
+            pltpu.SemaphoreType.DMA((count * PIECES,)),
         ]
         + kind.scratch(arrays),
-        compiler_params=pltpu.CompilerParams(collective_id=collective_id, has_side_effects=True),
+        compiler_params=pltpu.CompilerParams(
+            collective_id=collective_id, has_side_effects=True, vmem_limit_bytes=10 * 2**20
+        ),
         name="ring_gather",
     )(*shards, *arrays)
     full = [
@@ -329,20 +346,21 @@
             order.append(half + s)
     order.append(RING - 1)
 
+    pieces = halves([o.shape for o in out])
     mates = {}
 
     def trade(slot):
         d = goal(slot)
-        for w in range(count):
+        for p, (w, rows) in enumerate(pieces):
             copy = remote(
-                part[w].at[d // ZL, :, d % ZL, 1 - core],
-                mate[w].at[slot],
-                msend.at[w, slot],
-                mrecv.at[w, slot],
+                part[w].at[d // ZL, rows, d % ZL, 1 - core],
+                mate[w].at[slot, rows],
+                msend.at[p, slot],
+                mrecv.at[p, slot],
                 other,
             )
             copy.start()
-            mates[w, slot] = copy
+            mates[p, slot] = copy
 
     for slot in order[:4]:
         trade(slot)
@@ -352,28 +370,29 @@
     moves = {}
     for slot in order:
         d = goal(slot)
-        for w in range(count):
-            mates[w, slot].wait_recv()
-            total = part[w][d // ZL, :, d % ZL, core].astype(F32) + mate[w][slot].astype(F32)
+        for p, (w, rows) in enumerate(pieces):
+            mates[p, slot].wait_recv()
+            total = part[w][d // ZL, rows, d % ZL, core].astype(F32)
+            total = total + mate[w][slot, rows].astype(F32)
             if slot == RING - 1:
                 for last in (half - 1, RING - 2):
-                    moves[w, last].wait_recv()
-                    total = total + come[w][last].astype(F32)
-                out[w][...] = total
+                    moves[p, last].wait_recv()
+                    total = total + come[w][last, rows].astype(F32)
+                out[w][rows] = total
                 continue
             if slot not in (0, half):
-                moves[w, slot - 1].wait_recv()
-                total = total + come[w][slot - 1].astype(F32)
-            stage[w][slot] = total.astype(BF)
+                moves[p, slot - 1].wait_recv()
+                total = total + come[w][slot - 1, rows].astype(F32)
+            stage[w][slot, rows] = total.astype(BF)
             copy = remote(
-                stage[w].at[slot],
-                come[w].at[slot],
-                send.at[w, slot],
-                recv.at[w, slot],
+                stage[w].at[slot, rows],
+                come[w].at[slot, rows],
+                send.at[p, slot],
+                recv.at[p, slot],
                 right if slot < half else left,
             )
             copy.start()
-            moves[w, slot] = copy
+            moves[p, slot] = copy
         if slot < half:
             side.step(slot)
     side.finish()
@@ -400,10 +419,10 @@
         + [pltpu.VMEM((RING - 1,) + s, BF) for s in shards]
         + [pltpu.VMEM((RING - 1,) + s, BF) for s in shards]
         + [
-            pltpu.SemaphoreType.DMA((count, RING - 1)),
-            pltpu.SemaphoreType.DMA((count, RING - 1)),
-            pltpu.SemaphoreType.DMA((count, RING)),
-            pltpu.SemaphoreType.DMA((count, RING)),
+            pltpu.SemaphoreType.DMA((count * PIECES, RING - 1)),
+            pltpu.SemaphoreType.DMA((count * PIECES, RING - 1)),
+            pltpu.SemaphoreType.DMA((count * PIECES, RING)),
+            pltpu.SemaphoreType.DMA((count * PIECES, RING)),
         ]
         + kind.scratch(arrays),
         compiler_params=pltpu.CompilerParams(

time: 246 us -> 230 us (0.935)
  Pallas kernels: 208 us -> 202 us
  local copies, waits for them, and re-layouts: 18.6 us -> 12.9 us
    pallas_call x2, Pallas kernels: 111 us -> 104 us  [ring_gather(): pl.pallas_call(functools.partial(gather_kernel, count, kind, extra), out_...]
    unnamed x16 -> x14, local copies, waits for them, and re-layouts: 6.51 us -> 4.11 us
where the time goes in v3:
time: 230 us
  Pallas kernels  202 us (88%)
  matrix products  13.7 us (6%)
  local copies, waits for them, and re-layouts  12.9 us (6%)
    pallas_call x2, Pallas kernels, ring_gather(): pl.pallas_call(functools.partial(gather_kernel, count, kind, extra), out_...  104 us
    pallas_call x2, Pallas kernels, ring_scatter(): pl.pallas_call(functools.partial(scatter_kernel, count, kind, extra), out...  97.9 us
    dot_general x12, matrix products, contract(): return jnp.einsum(form, left, right, preferred_element_type=F32)  13.7 us

profile of v3, /device:TPU:6, one launch (start us, length us, event | category | flops | bytes accessed | tf_op | source)
XLA Modules:
  0.0 229.7 jit_solution(8057829299626985274)
XLA Ops:
  0.7 1.0 stack.27
  1.8 1.0 stack.28
  2.9 65.4 %ring_gather.2 = (bf16[2,2,8,2,16,1024]{5,4,3,2,1,0:T(8,128)(2,1)S(1)}, bf16[2,2,8,2,64,256]{5,4,3,2,1,0:T(8,128)(2,1)S(1)}, bf16[2,2,128,256]{3,2,1,0:T(8,128)(2,1)S(1)}) custom-call(bf16[2,16,1024]{2,1,0:T(8,128)(2,1)S(1)} %copy-done.2, bf16[2,64,256]{2,1,0:T(8,128)(2,1)S(1)} %copy-done.3, bf16[2,2,128,256]{3,2,1,0:T(8,128)(2,1)S(1)} %select_bitcast_fusion.1.refs_2_), custom_call_target="tpu_custom_call" | custom-call | tf_op jit(solution)/shard_map/ring_gather/pallas_call | solution.py:299
  68.4 0.7 convolution_convert_fusion.4
  69.1 1.2 copy.30
  70.4 0.9 convolution_convert_fusion.5
  71.3 1.2 copy.29
  72.6 38.7 %ring_gather.3 = (bf16[2,8,8,2,16,256]{5,4,3,2,1,0:T(8,128)(2,1)S(1)}, bf16[2,8,8,2,16,256]{5,4,3,2,1,0:T(8,128)(2,1)S(1)}, bf16[16,16,16,128]{3,2,1,0:T(8,128)(2,1)S(1)}, bf16[16,16,16,128]{3,2,1,0:T(8,128)(2,1)S(1)}) custom-call(bf16[8,16,256]{2,1,0:T(8,128)(2,1)S(1)} %copy-done, bf16[8,16,256]{2,1,0:T(8,128)(2,1)S(1)} %copy-done.1, ...), custom_call_target="tpu_custom_call" | custom-call | tf_op jit(solution)/shard_map/ring_gather/pallas_call | solution.py:299
  111.2 0.3 copy.31
  111.5 0.3 copy.32
  111.8 0.7 fusion.20
  112.5 2.2 fusion.6
  114.8 1.3 convolution_convert_fusion.7
  116.1 0.7 convolution_convert_fusion.6
  116.8 2.1 convolution_convert_fusion.3
  118.8 1.2 copy.36
  120.1 1.2 copy.35
  121.3 2.2 convolution_convert_fusion.2
  123.5 43.0 %ring_scatter.2 = (f32[8,16,256]{2,1,0:T(8,128)S(1)}, f32[8,16,256]{2,1,0:T(8,128)S(1)}, bf16[16,16,16,128]{3,2,1,0:T(8,128)(2,1)S(1)}, bf16[16,16,16,128]{3,2,1,0:T(8,128)(2,1)S(1)}) custom-call(bf16[2,8,8,2,16,256]{5,4,3,2,1,0:T(8,128)(2,1)} %bitcast.118, bf16[2,8,8,2,16,256]{5,4,3,2,1,0:T(8,128)(2,1)} %bitcast.130, ...), custom_call_target="tpu_custom_call" | custom-call | tf_op jit(solution)/shard_map/ring_scatter/pallas_call | solution.py:412
  166.5 0.3 copy.37
  166.8 0.6 convolution_convert_fusion.9
  167.4 0.3 copy.39
  167.7 0.8 convolution_convert_fusion.8
  168.6 0.8 convolution_convert_fusion.1
  169.4 0.7 convolution_convert_fusion
  170.1 54.8 %ring_scatter.3 = (f32[2,16,1024]{2,1,0:T(8,128)S(1)}, f32[2,64,256]{2,1,0:T(8,128)S(1)}, bf16[2,2,128,256]{3,2,1,0:T(8,128)(2,1)S(1)}) custom-call(bf16[2,2,8,2,16,1024]{5,4,3,2,1,0:T(8,128)(2,1)S(1)} %bitcast.96, bf16[2,2,8,2,64,256]{5,4,3,2,1,0:T(8,128)(2,1)S(1)} %bitcast.97, bf16[2,2,128,256]{3,2,1,0:T(8,128)(2,1)S(1)} %select_bitcast_fusion.refs_2_), custom_call_target="tpu_custom_call" | custom-call | tf_op jit(solution)/shard_map/ring_scatter/pallas_call | solution.py:412
  225.4 0.7 copy.51
  226.4 0.7 copy.50
  227.1 0.7 copy.56
  227.8 0.7 copy.57
  228.4 0.7 copy.58
  229.1 0.7 copy.59
  (19 shorter events, 1.0 us)
Async XLA Ops:
  0.6 2.3 %copy-start.3 = (bf16[2,64,256]{2,1,0:T(8,128)(2,1)S(1)}, bf16[2,64,256]{2,1,0:T(8,128)(2,1)}, u32[]{:S(2)}) copy-start(bf16[2,64,256]{2,1,0:T(8,128)(2,1)} %refs_1_.2) | copy-start | bytes 196612
  0.6 2.3 %copy-start.2 = (bf16[2,16,1024]{2,1,0:T(8,128)(2,1)S(1)}, bf16[2,16,1024]{2,1,0:T(8,128)(2,1)}, u32[]{:S(2)}) copy-start(bf16[2,16,1024]{2,1,0:T(8,128)(2,1)} %refs_0_.2) | copy-start | bytes 196612
  70.4 2.2 copy-start
  70.4 2.2 copy-start.1

commit v4 on v3

--- a/solution.py
+++ b/solution.py
@@ -54,7 +54,7 @@
 
 
 class Swap:
-    STEPS = (3,)
+    CUTS, LAG = 4, 3
     WAYS = (RING // 4, RING - RING // 4)
 
     @staticmethod
@@ -62,8 +62,8 @@
         shape = arrays[0].shape
         return [
             pltpu.VMEM(shape, BF),
-            pltpu.SemaphoreType.DMA((2, 2)),
-            pltpu.SemaphoreType.DMA((2, 2)),
+            pltpu.SemaphoreType.DMA((2, 2, Swap.CUTS)),
+            pltpu.SemaphoreType.DMA((2, 2, Swap.CUTS)),
         ]
 
     @staticmethod
@@ -80,33 +80,41 @@
     def peers(self):
         return self.targets
 
-    def start(self):
-        self.first = [
-            remote(
-                self.src.at[j], self.relay.at[j], self.send.at[0, j], self.recv.at[0, j], who
-            )
-            for j, who in enumerate(self.targets)
-        ]
-        for copy in self.first:
-            copy.start()
-
-    def step(self, s):
-        if s not in self.STEPS:
-            return
-        self.second = []
+    def cut(self, j, i):
+        kl, few = self.src.shape[1:3]
+        per = self.CUTS // kl
+        return j, i // per, pl.ds(i % per * (few // per), few // per)
+
+    def leg(self, src, dst, number, i):
+        copies = []
         for j, who in enumerate(self.targets):
-            self.first[j].wait_recv()
+            spot = self.cut(j, i)
             copy = remote(
-                self.relay.at[j], self.out.at[j], self.send.at[1, j], self.recv.at[1, j], who
+                src.at[spot], dst.at[spot], self.send.at[number, j, i], self.recv.at[number, j, i], who
             )
             copy.start()
-            self.second.append(copy)
+            copies.append(copy)
+        return copies
+
+    def start(self):
+        self.first = [self.leg(self.src, self.relay, 0, 0)]
+        self.second = []
+
+    def step(self, s):
+        if 1 <= s < self.CUTS:
+            self.first.append(self.leg(self.src, self.relay, 0, s))
+        if self.LAG <= s < self.LAG + self.CUTS:
+            for copy in self.first[s - self.LAG]:
+                copy.wait_recv()
+            self.second.append(self.leg(self.relay, self.out, 1, s - self.LAG))
 
     def finish(self):
-        for copy in self.second:
-            copy.wait_recv()
-        for copy in self.first + self.second:
-            copy.wait_send()
+        for copies in self.second:
+            for copy in copies:
+                copy.wait_recv()
+        for copies in self.first + self.second:
+            for copy in copies:
+                copy.wait_send()
 
 
 class Spread:
@@ -147,6 +155,10 @@
     def device(self, dy, dx):
         return at(self.z, self.core, (self.y + dy) % NY, (self.x + dx) % NX)
 
+    def route(self, j, w):
+        dy, dx, ry, rx = self.RELAYS[j]
+        return (dx, dy, rx, ry) if w % 2 else (dy, dx, ry, rx)
+
     def index(self, dy, dx):
         return (self.y + dy) % NY * NX + (self.x + dx) % NX
 
@@ -156,8 +168,9 @@
     def start(self):
         me = self.index(0, 0)
         self.sent, self.legs, self.keeps, self.comes = [], {}, [], []
-        for j, (dy, dx, ry, rx) in enumerate(self.RELAYS):
+        for j in range(len(self.RELAYS)):
             for w in range(self.n):
+                dy, dx, ry, rx = self.route(j, w)
                 copy = remote(
                     self.src[w].at[self.index(dy, dx)],
                     self.relay[w].at[j],
@@ -189,8 +202,8 @@
 
     def step(self, s):
         for j in self.STEPS.get(s, ()):
-            dy, dx, ry, rx = self.RELAYS[j]
             for w in range(self.n):
+                dy, dx, ry, rx = self.route(j, w)
                 self.legs[w, j].wait_recv()
                 self.sent.append(self.legs[w, j])
                 copy = remote(

time: 230 us -> 225 us (0.978)
  Pallas kernels: 202 us -> 196 us
    pallas_call x2, Pallas kernels: 97.9 us -> 94.2 us  [ring_scatter(): pl.pallas_call(functools.partial(scatter_kernel, count, kind, extra), out...]
where the time goes in v4:
time: 225 us; the launch traced here: 224 us
  Pallas kernels  196 us (87%)
  matrix products  13.7 us (6%)
  local copies, waits for them, and re-layouts  12.9 us (6%)
    pallas_call x2, Pallas kernels, ring_gather(): pl.pallas_call(functools.partial(gather_kernel, count, kind, extra), out_...  102 us
    pallas_call x2, Pallas kernels, ring_scatter(): pl.pallas_call(functools.partial(scatter_kernel, count, kind, extra), out...  94.2 us
    dot_general x12, matrix products, contract(): return jnp.einsum(form, left, right, preferred_element_type=F32)  13.7 us

profile of v4, /device:TPU:6, one launch (start us, length us, event | category | flops | bytes accessed | tf_op | source)
XLA Modules:
  0.0 223.8 jit_solution(7914075038156298998)
XLA Ops:
  0.7 1.0 stack.27
  1.8 1.0 stack.28
  2.9 62.7 %ring_gather.2 = (bf16[2,2,8,2,16,1024]{5,4,3,2,1,0:T(8,128)(2,1)S(1)}, bf16[2,2,8,2,64,256]{5,4,3,2,1,0:T(8,128)(2,1)S(1)}, bf16[2,2,128,256]{3,2,1,0:T(8,128)(2,1)S(1)}) custom-call(bf16[2,16,1024]{2,1,0:T(8,128)(2,1)S(1)} %copy-done.2, bf16[2,64,256]{2,1,0:T(8,128)(2,1)S(1)} %copy-done.3, bf16[2,2,128,256]{3,2,1,0:T(8,128)(2,1)S(1)} %select_bitcast_fusion.1.refs_2_), custom_call_target="tpu_custom_call" | custom-call | tf_op jit(solution)/shard_map/ring_gather/pallas_call | solution.py:312
  65.7 0.7 convolution_convert_fusion.4
  66.4 1.2 copy.30
  67.7 0.9 convolution_convert_fusion.5
  68.6 1.2 copy.29
  69.8 39.1 %ring_gather.3 = (bf16[2,8,8,2,16,256]{5,4,3,2,1,0:T(8,128)(2,1)S(1)}, bf16[2,8,8,2,16,256]{5,4,3,2,1,0:T(8,128)(2,1)S(1)}, bf16[16,16,16,128]{3,2,1,0:T(8,128)(2,1)S(1)}, bf16[16,16,16,128]{3,2,1,0:T(8,128)(2,1)S(1)}) custom-call(bf16[8,16,256]{2,1,0:T(8,128)(2,1)S(1)} %copy-done, bf16[8,16,256]{2,1,0:T(8,128)(2,1)S(1)} %copy-done.1, ...), custom_call_target="tpu_custom_call" | custom-call | tf_op jit(solution)/shard_map/ring_gather/pallas_call | solution.py:312
  109.0 0.3 copy.31
  109.3 0.3 copy.32
  109.6 0.7 fusion.20
  110.3 2.2 fusion.6
  112.5 1.3 convolution_convert_fusion.7
  113.8 0.7 convolution_convert_fusion.6
  114.5 2.1 convolution_convert_fusion.3
  116.6 1.2 copy.36
  117.8 1.2 copy.35
  119.0 2.2 convolution_convert_fusion.2
  121.2 40.8 %ring_scatter.2 = (f32[8,16,256]{2,1,0:T(8,128)S(1)}, f32[8,16,256]{2,1,0:T(8,128)S(1)}, bf16[16,16,16,128]{3,2,1,0:T(8,128)(2,1)S(1)}, bf16[16,16,16,128]{3,2,1,0:T(8,128)(2,1)S(1)}) custom-call(bf16[2,8,8,2,16,256]{5,4,3,2,1,0:T(8,128)(2,1)} %bitcast.118, bf16[2,8,8,2,16,256]{5,4,3,2,1,0:T(8,128)(2,1)} %bitcast.130, ...), custom_call_target="tpu_custom_call" | custom-call | tf_op jit(solution)/shard_map/ring_scatter/pallas_call | solution.py:425
  162.1 0.3 copy.37
  162.4 0.6 convolution_convert_fusion.9
  163.0 0.3 copy.39
  163.3 0.8 convolution_convert_fusion.8
  164.2 0.8 convolution_convert_fusion.1
  164.9 0.7 convolution_convert_fusion
  165.6 53.3 %ring_scatter.3 = (f32[2,16,1024]{2,1,0:T(8,128)S(1)}, f32[2,64,256]{2,1,0:T(8,128)S(1)}, bf16[2,2,128,256]{3,2,1,0:T(8,128)(2,1)S(1)}) custom-call(bf16[2,2,8,2,16,1024]{5,4,3,2,1,0:T(8,128)(2,1)S(1)} %bitcast.96, bf16[2,2,8,2,64,256]{5,4,3,2,1,0:T(8,128)(2,1)S(1)} %bitcast.97, bf16[2,2,128,256]{3,2,1,0:T(8,128)(2,1)S(1)} %select_bitcast_fusion.refs_2_), custom_call_target="tpu_custom_call" | custom-call | tf_op jit(solution)/shard_map/ring_scatter/pallas_call | solution.py:425
  219.4 0.7 copy.51
  220.4 0.7 copy.50
  221.2 0.7 copy.56
  221.8 0.7 copy.57
  222.5 0.7 copy.58
  223.1 0.7 copy.59
  (19 shorter events, 1.0 us)
Async XLA Ops:
  0.6 2.3 %copy-start.3 = (bf16[2,64,256]{2,1,0:T(8,128)(2,1)S(1)}, bf16[2,64,256]{2,1,0:T(8,128)(2,1)}, u32[]{:S(2)}) copy-start(bf16[2,64,256]{2,1,0:T(8,128)(2,1)} %refs_1_.2) | copy-start | bytes 196612
  0.6 2.3 %copy-start.2 = (bf16[2,16,1024]{2,1,0:T(8,128)(2,1)S(1)}, bf16[2,16,1024]{2,1,0:T(8,128)(2,1)}, u32[]{:S(2)}) copy-start(bf16[2,16,1024]{2,1,0:T(8,128)(2,1)} %refs_0_.2) | copy-start | bytes 196612
  67.6 2.2 copy-start
  67.6 2.2 copy-start.1
